TPU v7x, 32 devices: a whole 2x2x4 slice. The times are simulated.
32 devices in a mesh: dp: 2 (over core), seq: 4 (over z), tensor: 4 (over y, x).
Axes of the slice: x: 2, y: 2, z: 4, core: 2. Of those that a mesh axis runs over, the one named last changes fastest.
Arguments:
- tokens: bfloat16 [4, 4096, 1024], P('dp', ('seq', 'tensor')), may hold values from -6 to 6
- w_query: bfloat16 [1024, 1024], replicated, may hold values from -0.1875 to 0.1875
- w_key: bfloat16 [1024, 1024], replicated, may hold values from -0.1875 to 0.1875
- w_value: bfloat16 [1024, 1024], replicated, may hold values from -0.1875 to 0.1875
- w_ugate: bfloat16 [1024, 1024], replicated, may hold values from -0.1875 to 0.1875
- w_output: bfloat16 [1024, 1024], replicated, may hold values from -0.1875 to 0.1875
- w_left: bfloat16 [1024, 2816], P(None, 'tensor'), may hold values from -0.1875 to 0.1875
- w_right: bfloat16 [1024, 2816], P(None, 'tensor'), may hold values from -0.1875 to 0.1875
- w_down: bfloat16 [2816, 1024], P('tensor'), may hold values from -0.109375 to 0.109375
- decay_rate: float32 [8], replicated, may hold values from 0.00012207031 to 0.05
- cotangent: bfloat16 [4, 4096, 1024], P('dp', ('seq', 'tensor')), may hold values from -6 to 6
Outputs:
- mixed_out: bfloat16 [4, 4096, 1024], P('dp', ('seq', 'tensor'))
- grad_tokens: float32 [4, 4096, 1024], P('dp', ('seq', 'tensor'))
- grad_query: float32 [1024, 1024], replicated
- grad_key: float32 [1024, 1024], replicated
- grad_value: float32 [1024, 1024], replicated
- grad_ugate: float32 [1024, 1024], replicated
- grad_output: float32 [1024, 1024], replicated
- grad_left: float32 [1024, 2816], P(None, 'tensor')
- grad_right: float32 [1024, 2816], P(None, 'tensor')
- grad_down: float32 [2816, 1024], P('tensor')
All inputs are finite; a program needn't handle non-finite values.
Results may differ from a plain program's by a relative error of at most 0.017.
Values may be sent and summed in bfloat16 or wider, within the bound.
A program may use at most 320 MiB of HBM per device.

v0:
```python
import jax
import jax.numpy as jnp
from jax import lax
from jax.sharding import PartitionSpec as P

EPS = 1e-06


def prefix(value, axis, join, neutral, backward):
    count, mine = (lax.axis_size(axis), lax.axis_index(axis))
    pieces = jax.tree.map(lambda part: lax.all_gather(part, axis), value)
    if backward:
        pieces = jax.tree.map(lambda part: part[::-1], pieces)
        mine = count - 1 - mine
    total = jax.tree.map(
        lambda part, zero: jnp.full_like(part, 0) + jnp.asarray(zero, part.dtype), value, neutral
    )

    def hop(position, total):
        longer = join(total, jax.tree.map(lambda part: part[position], pieces))
        return jax.tree.map(lambda new, old: jnp.where(position < mine, new, old), longer, total)

    return lax.fori_loop(0, count - 1, hop, total)


def norm_rows(values):
    inv_scale = lax.rsqrt(jnp.mean(values * values, axis=-1, keepdims=True) + EPS)
    return (values * inv_scale, inv_scale)


def norm_back(gradient, normed, inv_scale):
    return inv_scale * (gradient - normed * jnp.mean(gradient * normed, axis=-1, keepdims=True))


def rotate(values, cosine, sine_part):
    half_dim = values.shape[-1] // 2
    first_half = values[..., :half_dim]
    second_half = values[..., half_dim:]
    return jnp.concatenate(
        [
            first_half * cosine - second_half * sine_part,
            second_half * cosine + first_half * sine_part,
        ],
        axis=-1,
    )


def rotate_back(values, cosine, sine_part):
    half_dim = values.shape[-1] // 2
    first_half = values[..., :half_dim]
    second_half = values[..., half_dim:]
    return jnp.concatenate(
        [
            first_half * cosine + second_half * sine_part,
            second_half * cosine - first_half * sine_part,
        ],
        axis=-1,
    )


def split_heads(values, head_count):
    seq_count, group_len, model_width = values.shape
    return values.reshape(seq_count, group_len, head_count, model_width // head_count).transpose(
        0, 2, 1, 3
    )


def join_heads(values):
    seq_count, head_count, group_len, head_dim = values.shape
    return values.transpose(0, 2, 1, 3).reshape(seq_count, group_len, head_count * head_dim)


def project(inputs, matrix):
    return jnp.einsum("scd,de->sce", inputs, matrix, preferred_element_type=jnp.float32)


def project_back(gradient, matrix):
    return jnp.einsum("sce,de->scd", gradient, matrix, preferred_element_type=jnp.float32)


def weight_grad(inputs, gradient):
    return jnp.einsum("scd,sce->de", inputs, gradient, preferred_element_type=jnp.float32)


def silu_slope(values):
    sigmoid_v = jax.nn.sigmoid(values)
    return sigmoid_v * (1.0 + values * (1.0 - sigmoid_v))


def carry_combine(earlier, latter):
    return (earlier[0] * latter[0], latter[0] * earlier[1] + latter[1])


def on_device(
    tokens,
    w_query,
    w_key,
    w_value,
    w_ugate,
    w_output,
    w_left,
    w_right,
    w_down,
    decay_rate,
    cotangent,
):
    seq_count, group_len, model_width = tokens.shape
    head_count = decay_rate.shape[0]
    head_dim = model_width // head_count
    half_dim = head_dim // 2
    hidden = w_left.shape[1]
    row_count = seq_count * group_len
    position_block = lax.axis_index(("seq", "tensor"))
    places = (position_block * group_len + jnp.arange(group_len)).astype(jnp.float32)
    frequency = 10000.0 ** (-jnp.arange(half_dim, dtype=jnp.float32) / half_dim)
    angles = places[:, None] * frequency[None, :]
    cosine = jnp.cos(angles)
    sine_part = jnp.sin(angles)
    step_pos = jnp.arange(group_len, dtype=jnp.float32)
    lag_steps = step_pos[:, None] - step_pos[None, :]
    decay_mask = jnp.where(
        lag_steps >= 0, jnp.exp(-decay_rate[:, None, None] * jnp.maximum(lag_steps, 0.0)), 0.0
    )
    query_weight = jnp.exp(-decay_rate[:, None] * (step_pos + 1.0))[:, :, None]
    key_weight = jnp.exp(-decay_rate[:, None] * (group_len - 1.0 - step_pos))[:, :, None]
    carry_decay = jnp.exp(-decay_rate * group_len)[:, None, None]
    inputs = tokens.astype(jnp.float32)
    normed_one, scale_one = norm_rows(inputs)
    normed_low = normed_one.astype(jnp.bfloat16)
    query_pre = project(normed_low, w_query)
    key_pre = project(normed_low, w_key)
    value_pre = project(normed_low, w_value)
    ugate = project(normed_low, w_ugate)
    query_rot = rotate(split_heads(jax.nn.silu(query_pre), head_count), cosine, sine_part)
    key_rot = rotate(split_heads(jax.nn.silu(key_pre), head_count), cosine, sine_part)
    query_low = query_rot.astype(jnp.bfloat16)
    key_low = key_rot.astype(jnp.bfloat16)
    value_low = split_heads(value_pre, head_count).astype(jnp.bfloat16)
    query_dec = (query_rot * query_weight).astype(jnp.bfloat16)
    key_dec = (key_rot * key_weight).astype(jnp.bfloat16)
    scores = jnp.einsum("shie,shje->shij", query_low, key_low, preferred_element_type=jnp.float32)
    weights_low = (scores * decay_mask).astype(jnp.bfloat16)
    inner_part = jnp.einsum(
        "shij,shje->shie", weights_low, value_low, preferred_element_type=jnp.float32
    )
    local_state = jnp.einsum(
        "shje,shjf->shef", key_dec, value_low, preferred_element_type=jnp.float32
    )
    identity = (jnp.ones_like(carry_decay), jnp.zeros_like(local_state))
    carried = prefix((carry_decay, local_state), ("seq", "tensor"), carry_combine, identity, False)
    state_in = carried[1]
    state_low = state_in.astype(jnp.bfloat16)
    outer_part = jnp.einsum(
        "shie,shef->shif", query_dec, state_low, preferred_element_type=jnp.float32
    )
    merged = join_heads(inner_part + outer_part)
    normed_att, scale_att = norm_rows(merged)
    gated_low = (normed_att * ugate).astype(jnp.bfloat16)
    branch = project(gated_low, w_output)
    residual = inputs + branch
    normed_two, scale_two = norm_rows(residual)
    normed_flat = normed_two.astype(jnp.bfloat16).reshape(row_count, model_width)
    w_pair = jnp.concatenate([w_left, w_right], axis=1)
    pair_all = jnp.dot(
        lax.all_gather(normed_flat, "tensor", axis=0, tiled=True),
        w_pair,
        preferred_element_type=jnp.float32,
    )
    left_half = pair_all[:, :hidden]
    right_half = pair_all[:, hidden:]
    product_low = (left_half * right_half).astype(jnp.bfloat16)
    ffn_rows = lax.psum_scatter(
        jnp.dot(product_low, w_down, preferred_element_type=jnp.float32).astype(jnp.bfloat16),
        "tensor",
        scatter_dimension=0,
        tiled=True,
    ).astype(jnp.float32)
    mixed_out = (residual + ffn_rows.reshape(seq_count, group_len, model_width)).astype(
        jnp.bfloat16
    )
    grad_res = cotangent.astype(jnp.float32)
    grad_low = grad_res.reshape(row_count, model_width).astype(jnp.bfloat16)
    grad_all = lax.all_gather(grad_low, "tensor", axis=0, tiled=True)
    grad_product = jnp.einsum("rd,fd->rf", grad_all, w_down, preferred_element_type=jnp.float32)
    grad_down = jnp.einsum("rf,rd->fd", product_low, grad_all, preferred_element_type=jnp.float32)
    grad_pair = jnp.concatenate(
        [grad_product * right_half, grad_product * left_half], axis=1
    ).astype(jnp.bfloat16)
    grad_normed_two = lax.psum_scatter(
        jnp.einsum("rf,df->rd", grad_pair, w_pair, preferred_element_type=jnp.float32),
        "tensor",
        scatter_dimension=0,
        tiled=True,
    )
    pair_grad = jnp.einsum(
        "rd,rf->df",
        lax.all_gather(normed_flat, "tensor", axis=0, tiled=True),
        grad_pair,
        preferred_element_type=jnp.float32,
    )
    grad_left = pair_grad[:, :hidden]
    grad_right = pair_grad[:, hidden:]
    grad_mid = grad_res + norm_back(
        grad_normed_two.reshape(seq_count, group_len, model_width), normed_two, scale_two
    )
    grad_branch = grad_mid.astype(jnp.bfloat16)
    grad_gated = project_back(grad_branch, w_output)
    grad_output = weight_grad(gated_low, grad_branch)
    grad_ugate_pre = (grad_gated * normed_att).astype(jnp.bfloat16)
    grad_merged = norm_back(grad_gated * ugate, normed_att, scale_att)
    grad_att = split_heads(grad_merged, head_count).astype(jnp.bfloat16)
    grad_weights = jnp.einsum(
        "shie,shje->shij", grad_att, value_low, preferred_element_type=jnp.float32
    )
    grad_value_heads = jnp.einsum(
        "shij,shie->shje", weights_low, grad_att, preferred_element_type=jnp.float32
    )
    grad_scores = (grad_weights * decay_mask).astype(jnp.bfloat16)
    grad_query_rot = jnp.einsum(
        "shij,shje->shie", grad_scores, key_low, preferred_element_type=jnp.float32
    )
    grad_key_rot = jnp.einsum(
        "shij,shie->shje", grad_scores, query_low, preferred_element_type=jnp.float32
    )
    grad_query_dec = jnp.einsum(
        "shif,shef->shie", grad_att, state_low, preferred_element_type=jnp.float32
    )
    grad_state_in = jnp.einsum(
        "shie,shif->shef", query_dec, grad_att, preferred_element_type=jnp.float32
    )
    carried_back = prefix(
        (carry_decay, grad_state_in), ("seq", "tensor"), carry_combine, identity, True
    )
    grad_local = carried_back[1]
    grad_local_low = grad_local.astype(jnp.bfloat16)
    grad_key_dec = jnp.einsum(
        "shef,shjf->shje", grad_local_low, value_low, preferred_element_type=jnp.float32
    )
    grad_value_heads = grad_value_heads + jnp.einsum(
        "shje,shef->shjf", key_dec, grad_local_low, preferred_element_type=jnp.float32
    )
    grad_query_rot = grad_query_rot + grad_query_dec * query_weight
    grad_key_rot = grad_key_rot + grad_key_dec * key_weight
    grad_query_pre = (
        join_heads(rotate_back(grad_query_rot, cosine, sine_part)) * silu_slope(query_pre)
    ).astype(jnp.bfloat16)
    grad_key_pre = (
        join_heads(rotate_back(grad_key_rot, cosine, sine_part)) * silu_slope(key_pre)
    ).astype(jnp.bfloat16)
    grad_value_pre = join_heads(grad_value_heads).astype(jnp.bfloat16)
    grad_normed_one = (
        project_back(grad_query_pre, w_query)
        + project_back(grad_key_pre, w_key)
        + project_back(grad_value_pre, w_value)
        + project_back(grad_ugate_pre, w_ugate)
    )
    grad_tokens = grad_mid + norm_back(grad_normed_one, normed_one, scale_one)
    grad_query = weight_grad(normed_low, grad_query_pre)
    grad_key = weight_grad(normed_low, grad_key_pre)
    grad_value = weight_grad(normed_low, grad_value_pre)
    grad_ugate = weight_grad(normed_low, grad_ugate_pre)
    grad_query, grad_key, grad_value, grad_ugate, grad_output = lax.psum(
        (grad_query, grad_key, grad_value, grad_ugate, grad_output), ("dp", "seq", "tensor")
    )
    grad_left, grad_right, grad_down = (
        lax.psum(grad_left.astype(jnp.bfloat16), ("dp", "seq")).astype(jnp.float32),
        lax.psum(grad_right.astype(jnp.bfloat16), ("dp", "seq")).astype(jnp.float32),
        lax.psum(grad_down.astype(jnp.bfloat16), ("dp", "seq")).astype(jnp.float32),
    )
    return (
        mixed_out,
        grad_tokens,
        grad_query,
        grad_key,
        grad_value,
        grad_ugate,
        grad_output,
        grad_left,
        grad_right,
        grad_down,
    )


def solution(mesh):
    return jax.shard_map(
        on_device,
        mesh=mesh,
        in_specs=(
            P("dp", ("seq", "tensor"), None),
            P(),
            P(),
            P(),
            P(),
            P(),
            P(None, "tensor"),
            P(None, "tensor"),
            P("tensor", None),
            P(),
            P("dp", ("seq", "tensor"), None),
        ),
        out_specs=(
            P("dp", ("seq", "tensor"), None),
            P("dp", ("seq", "tensor"), None),
            P(),
            P(),
            P(),
            P(),
            P(),
            P(None, "tensor"),
            P(None, "tensor"),
            P("tensor", None),
        ),
        check_vma=False,
    )
```

profile of v0, /device:TPU:0, one launch (start us, length us, event | category | flops | bytes accessed | tf_op | source)
XLA Modules:
  0.0 1207.8 jit_solution(17854684559947694874)
XLA Ops:
  7.3 1.6 fusion.10
  8.9 3.2 fusion.29
  12.2 1.9 bitcast_bitcast_fusion
  18.3 1.9 bitcast_bitcast_fusion.1
  20.2 3.0 fusion.39
  25.2 3.1 multiply_subtract_fusion.2
  31.9 2.5 copy.146
  34.4 45.2 %all-reduce = f32[128]{0:T(128)S(1)} all-reduce(f32[128]{0:T(128)S(1)} %get-tuple-element.350), channel_id=2, replica_groups=mesh['dp'=2,'seq'=4,'tensor'=4] {'seq','tensor'}, use_global_device_ids=true, to_apply=%add | all-reduce | flops 128 | bytes 1024
  79.9 4.6 fusion.48
  84.6 1.9 multiply_convert_fusion.9
  89.6 2.1 fusion.43
  91.8 134.5 %all-gather.12.cloned.1.call-done = f32[32,8,128,128]{3,2,1,0:T(8,128)} async-done(((f32[2,8,128,128]{3,2,1,0:T(8,128)}), f32[32,8,128,128]{3,2,1,0:T(8,128)}) %all-gather.12.cloned.1.call-update) | async-done | bytes 16777232 | tf_op jit(solution)/shard_map/all_gather | solution.py:11
  226.3 23.3 %while.28 = (s32[]{:T(128)}, f32[2,8,128,128]{3,2,1,0:T(8,128)S(1)}, s32[]{:T(128)}, f32[16,8,1,1]{1,3,2,0:T(1,128)S(1)}, f32[16,2,8,128,128]{4,3,2,1,0:T(8,128)}, /*index=5*/s32[]{:T(128)}, s32[]{:T(128)}) while((s32[]{:T(128)}, f32[2,8,128,128]{3,2,1,0:T(8,128)S(1)}, s32[]{:T(128)}, f32[16,8,1,1]{1,3,2,0:T(1,128)S(1)}, ...), condition=%wide.region_2.3_spmd.clone, body=%wide.region_1.2_spmd.clone.sunk | while | flops 1048580 | bytes 3145929 | solution.py:23
  249.6 3.7 fusion.22
  253.3 2.9 copy.92
  256.2 5.2 multiply_convert_fusion.7
  266.3 2.7 constant_dynamic-update-slice_fusion.1
  270.2 46.0 %all-gather.8.cloned.1.call-done = bf16[2048,1024]{1,0:T(8,128)(2,1)} async-done(((bf16[512,1024]{1,0:T(8,128)(2,1)}), bf16[2048,1024]{1,0:T(8,128)(2,1)}) %all-gather.8.cloned.1.call-update) | async-done | bytes 4194320 | tf_op jit(solution)/shard_map/all_gather | solution.py:165
  316.3 11.5 fusion.69
  327.8 43.0 %all-gather.10.cloned.1.call-done = bf16[2048,1024]{1,0:T(8,128)(2,1)} async-done(((bf16[512,1024]{1,0:T(8,128)(2,1)}), bf16[2048,1024]{1,0:T(8,128)(2,1)}) %all-gather.10.cloned.1.call-update) | async-done | bytes 4194320 | tf_op jit(solution)/shard_map/all_gather | solution.py:183
  370.7 10.9 multiply_convert_fusion.1
  381.7 1.6 copy-done.60
  384.2 10.7 fusion.2
  395.2 7.7 convolution_convert_fusion.1
  403.0 78.4 %reduce-scatter.5.cloned.1.call-done = f32[512,1024]{1,0:T(8,128)} async-done(((f32[2048,1024]{1,0:T(8,128)}), f32[512,1024]{1,0:T(8,128)}) %reduce-scatter.5.cloned.1.call-update) | async-done | bytes 2097168 | tf_op jit(solution)/shard_map/reduce_scatter | solution.py:189
  481.3 2.6 multiply_reduce_fusion.1
  483.9 53.4 %reduce-scatter.3.cloned.1.call-done = bf16[512,1024]{1,0:T(8,128)(2,1)} async-done(((bf16[2048,1024]{1,0:T(8,128)(2,1)}), bf16[512,1024]{1,0:T(8,128)(2,1)}) %reduce-scatter.3.cloned.1.call-update) | async-done | bytes 1048592 | tf_op jit(solution)/shard_map/reduce_scatter | solution.py:172
  537.3 4.5 multiply_add_fusion.4
  541.9 2.6 multiply_reduce_fusion
  545.8 1.6 copy.140
  549.4 10.4 convolution_convert_fusion
  559.8 2.4 fusion.68
  563.1 4.3 convolution_convert_fusion.2
  567.5 2.8 multiply_convert_fusion.3
  570.3 2.1 fusion.71
  574.3 3.3 convolution_bitcast_fusion
  577.6 1.8 fusion.73
  579.4 2.2 multiply_add_fusion.3
  581.5 3.4 convolution_bitcast_fusion.1
  584.9 155.1 %all-gather.14.cloned.1.call-done = f32[32,8,128,128]{3,2,1,0:T(8,128)} async-done(((f32[2,8,128,128]{3,2,1,0:T(8,128)}), f32[32,8,128,128]{3,2,1,0:T(8,128)}) %all-gather.14.cloned.1.call-update) | async-done | bytes 16777232 | tf_op jit(solution)/shard_map/all_gather | solution.py:11
  740.0 11.9 rev.7
  751.9 23.4 %while.29 = (s32[]{:T(128)}, f32[2,8,128,128]{3,2,1,0:T(8,128)S(1)}, s32[]{:T(128)}, f32[16,8,1,1]{1,3,2,0:T(1,128)S(1)}, f32[16,2,8,128,128]{4,3,2,1,0:T(8,128)}, /*index=5*/s32[]{:T(128)}, s32[]{:T(128)}) while((s32[]{:T(128)}, f32[2,8,128,128]{3,2,1,0:T(8,128)S(1)}, s32[]{:T(128)}, f32[16,8,1,1]{1,3,2,0:T(1,128)S(1)}, ...), condition=%wide.region_10.11_spmd.clone, body=%wide.region_9.10_spmd.clone.sunk | while | flops 1048580 | bytes 3145929 | solution.py:23
  753.5 1.5 fusion.116
  755.0 1.5 fusion.116
  775.3 2.6 multiply_add_fusion.1
  777.9 2.0 multiply_add_fusion.2
  781.1 3.4 convolution_bitcast_fusion.4
  785.6 3.4 convolution_bitcast_fusion.3
  790.4 3.5 convolution_bitcast_fusion.2
  794.0 51.4 %all-reduce.8.cloned.1.call-done = (bf16[1024,704]{1,0:T(8,128)(2,1)}, bf16[1024,704]{1,0:T(8,128)(2,1)}, bf16[704,1024]{1,0:T(8,128)(2,1)}) async-done(((bf16[1024,704]{1,0:T(8,128)(2,1)}, bf16[1024,704]{1,0:T(8,128)(2,1)}, bf16[704,1024]{1,0:T(8,128)(2,1)}), (bf16[1024,704]{1,0:T(8,128)(2,1)}, bf16[1024,704]{1,0:T(8,128)(2,1)}, bf16[704,1024]{1,0:T(8,128)(2,1)})) %all-reduce.8.cloned.1.call-update) | async-done | bytes 4325392 | tf_op jit(solution)/shard_map/psum | solution.py:266
  845.4 3.4 convert_element_type.148
  848.8 2.0 copy.115
  850.8 3.3 copy.116
  854.1 2.7 fusion.18
  863.0 1.8 fusion.9
  864.8 316.8 %all-reduce.6.cloned.1.call-done = (f32[1024,1024]{1,0:T(8,128)}, f32[1024,1024]{1,0:T(8,128)}, f32[1024,1024]{1,0:T(8,128)}, f32[1024,1024]{1,0:T(8,128)}, f32[1024,1024]{1,0:T(8,128)}) async-done(((f32[1024,1024]{1,0:T(8,128)}, f32[1024,1024]{1,0:T(8,128)}, f32[1024,1024]{1,0:T(8,128)}, f32[1024,1024]{1,0:T(8,128)}, f32[1024,1024]{1,0:T(8,128)}), (f32[1024,1024]{1,0:T(8,128)}, f32[1024,1024]{1,0:T(8,128)}, ...) | async-done | bytes 20971536 | tf_op jit(solution)/shard_map/psum | solution.py:262
  1181.6 4.9 copy.187
  1186.6 2.1 copy.188
  1188.7 1.6 copy-done.39
  1190.3 2.1 copy.189
  1192.4 1.6 copy-done.38
  1194.0 2.1 copy.190
  1196.1 1.6 copy-done.37
  1197.7 2.1 copy.191
  (232 shorter events, 79.7 us)
Async XLA Ops:
  7.2 254.3 %copy-start = (bf16[1024,1024]{1,0:T(8,128)(2,1)S(1)}, bf16[1024,1024]{1,0:T(8,128)(2,1)}, u32[]{:S(2)}) copy-start(bf16[1024,1024]{1,0:T(8,128)(2,1)} %param.20) | copy-start | bytes 6291460
  7.2 219.1 %all-gather.12.cloned.1.call-start = ((), (), s32[]{:S(2)}) async-start(), calls=%async_computation.6 | async-start | bytes 17825792 | tf_op jit(solution)/shard_map/all_gather | solution.py:11
  12.1 2.1 copy-start.29
  12.1 2.1 copy-start.17
  12.2 3.4 copy-start.43
  16.9 1.4 copy-start.31
  20.1 3.6 copy-start.58
  20.1 4.9 copy-start.54
  20.1 5.0 copy-start.15
  20.1 5.0 copy-start.16
  23.2 6.1 copy-start.21
  28.3 2.0 copy-start.13
  30.3 1.5 copy-start.22
  31.9 284.4 %all-gather.8.cloned.1.call-start = ((), (), s32[]{:S(2)}) async-start(), calls=%async_computation.2 | async-start | bytes 5242880 | tf_op jit(solution)/shard_map/all_gather | solution.py:165
  79.8 4.6 copy-start.10
  79.8 4.7 copy-start.11
  84.4 2.6 copy-start.24
  84.5 2.6 copy-start.26
  84.6 2.0 copy-start.41
  87.0 1.3 copy-start.3
  256.2 5.3 copy-start.18
  261.5 1.4 copy-start.47
  265.4 105.4 %all-gather.10.cloned.1.call-start = ((), (), s32[]{:S(2)}) async-start(), calls=%async_computation.4 | async-start | bytes 5242880 | tf_op jit(solution)/shard_map/all_gather | solution.py:183
  266.1 215.2 %reduce-scatter.5.cloned.1.call-start = ((), (), s32[]{:S(2)}) async-start(), calls=%async_computation.5 | async-start | bytes 10485760 | tf_op jit(solution)/shard_map/reduce_scatter | solution.py:189
  266.3 2.7 copy-start.46
  381.7 1.6 copy-start.60
  381.7 2.5 copy-start.61
  394.9 142.4 %reduce-scatter.3.cloned.1.call-start = ((), (), s32[]{:S(2)}) async-start(), calls=%async_computation.3 | async-start | bytes 5242880 | tf_op jit(solution)/shard_map/reduce_scatter | solution.py:172
  402.9 337.1 %all-gather.14.cloned.1.call-start = ((), (), s32[]{:S(2)}) async-start(), calls=%async_computation.7 | async-start | bytes 17825792 | tf_op jit(solution)/shard_map/all_gather | solution.py:11
  537.3 4.5 copy-start.2
  537.3 4.5 copy-start.33
  541.9 2.6 copy-start.6
  545.8 1.6 copy-start.28
  548.9 296.5 %all-reduce.8.cloned.1.call-start = ((), (), s32[]{:S(2)}) async-start(), calls=%async_computation.9 | async-start | bytes 9175040 | tf_op jit(solution)/shard_map/psum | solution.py:266
  549.4 12.8 %copy-start.59 = (bf16[2048,704]{0,1:T(8,128)(2,1)S(1)}, bf16[2048,704]{0,1:T(8,128)(2,1)}, u32[]{:S(2)}) copy-start(bf16[2048,704]{0,1:T(8,128)(2,1)} %get-tuple-element.328) | copy-start | bytes 8650756
  559.8 3.3 copy-start.55
  567.5 614.2 %all-reduce.6.cloned.1.call-start = ((), (), s32[]{:S(2)}) async-start(), calls=%async_computation.8 | async-start | bytes 41943040 | tf_op jit(solution)/shard_map/psum | solution.py:262
  567.5 2.8 copy-start.27
  570.3 2.1 copy-start.25
  572.4 1.6 copy-start.7
  572.4 1.9 copy-start.48
  574.3 3.3 copy-start.5
  579.4 2.2 copy-start.19
  579.4 2.2 copy-start.53
  775.3 2.6 copy-start.14
  777.9 2.0 copy-start.32
  781.1 3.4 copy-start.35
  781.1 3.4 copy-start.30
  785.5 3.4 copy-start.49
  785.5 3.4 copy-start.23
  785.5 3.4 copy-start.34
  845.4 3.4 copy-start.45
  850.8 3.3 copy-start.42
  854.1 2.7 copy-start.50
  854.1 2.7 copy-start.56
  856.8 2.6 copy-start.57
  859.4 1.3 copy-start.36
  859.4 2.0 copy-start.44
  861.4 1.6 copy-start.8
  1181.6 4.9 copy-start.40
  1186.6 3.7 copy-start.39
  1190.3 3.7 copy-start.38
  1194.0 3.7 copy-start.37
  1197.7 3.1 copy-start.1
  (6 other events, 7.5 us)
Sparse Core Ops, SparseCore 0:
  32.0 194.2 all-gather.11
  265.5 50.7 all-gather.7
  318.1 52.5 all-gather.9
  395.0 86.2 reduce-scatter.4
  484.7 52.5 reduce-scatter.2
  549.0 190.9 all-gather.13
  743.2 102.1 all-reduce.7
  852.4 329.1 all-reduce.5
where the time goes:
time: 1220 us; the launch traced here: 1210 us
  waiting for transfers between devices  879 us (72%)
  matrix products  118 us (10%)
  other arithmetic  81.4 us (7%)
  local copies, waits for them, and re-layouts  65.8 us (5%)
  blocking collectives  45.2 us (4%)
  between operations  15.7 us (1%)
    psum x1, waiting for transfers between devices, on_device(): lax.psum((grad_query, grad_key, grad_value, grad_ugate, grad_output), ('d...  317 us
    all_gather x2, waiting for transfers between devices, prefix(): pieces = jax.tree.map(lambda part: lax.all_gather(part, axis), value)  290 us
    reduce_scatter x1, waiting for transfers between devices, on_device(): lax.psum_scatter(jnp.einsum('rf,df->rd', grad_pair, w_pair, preferred_ele...  78.4 us
    reduce_scatter x1, waiting for transfers between devices, on_device(): lax.psum_scatter(jnp.dot(product_low, w_down, preferred_element_type=jnp....  53.4 us
    psum x1, waiting for transfers between devices, on_device(): lax.psum(grad_left.astype(jnp.bfloat16), ('dp', 'seq')).astype(jnp.float32)  51.4 us
    all_gather x1, waiting for transfers between devices, on_device(): lax.all_gather(normed_flat, 'tensor', axis=0, tiled=True)  46 us
    unnamed x135, local copies, waits for them, and re-layouts  45.5 us
    select_n x30, other arithmetic, hop(): jnp.where(position < mine, new, old)  45.5 us
  transfers between devices with their start and end apart: 8, of which 8 were waited for; matrix products, arithmetic and copies ran while one was open for 12% of the time, Pallas kernels for 0%

commit v1 on v0

v1 whole, which is shorter than its diff:
```python
import jax
import jax.numpy as jnp
from jax import lax
from jax.sharding import PartitionSpec as P

EPS = 1e-06
F32 = jnp.float32
BF16 = jnp.bfloat16


def swap(value, axis, bit):
    count = lax.axis_size(axis)
    return jax.tree.map(
        lambda v: lax.ppermute(v, axis, [(i, i ^ bit) for i in range(count)]), value
    )


def shift(value, axis, step):
    count = lax.axis_size(axis)
    pairs = [(i, i + step) for i in range(count) if 0 <= i + step < count]
    return lax.ppermute(value, axis, pairs)


def take_half(value, which, axis=0):
    half = value.shape[axis] // 2
    return lax.dynamic_slice_in_dim(value, which * half, half, axis)


def join_half(mine, other, which, axis=0):
    return jnp.where(
        which == 0,
        jnp.concatenate([mine, other], axis=axis),
        jnp.concatenate([other, mine], axis=axis),
    )


def carried_state(local, decay_rate, block_len, backward):
    heads = local.shape[1]
    width = lax.axis_size("tensor")
    share = heads // width
    depth = lax.axis_size("seq")
    mine = lax.axis_index("tensor")

    def power(count, rate):
        return jnp.exp(-rate * block_len * count)

    pieces = []
    for b in range(width):
        part = lax.dynamic_slice_in_dim(local, (mine ^ b) * share, share, 1)
        pieces.append(part if b == 0 else swap(part.astype(BF16), "tensor", b).astype(F32))
    rate = lax.dynamic_slice_in_dim(decay_rate, mine * share, share, 0)

    def scaled(coef, part):
        return coef[None, :, None, None] * part

    total = 0.0
    for b in range(width):
        place = mine ^ b
        left = place if backward else width - 1 - place
        total = total + scaled(power(left.astype(F32), rate), pieces[b])
    total_low = total.astype(BF16)
    entering = 0.0
    for j in range(1, depth):
        step = -j if backward else j
        moved = shift(total_low, "seq", step).astype(F32)
        entering = entering + scaled(power(float(width * (j - 1)), rate), moved)
    outs = []
    for d in range(width):
        target = mine ^ d
        inner = (width - 1 - target) if backward else target
        value = scaled(power(inner.astype(F32), rate), entering)
        for b in range(width):
            if b == d:
                continue
            source = mine ^ b
            gap = (source - target - 1) if backward else (target - source - 1)
            coef = jnp.where(gap >= 0, power(jnp.maximum(gap, 0).astype(F32), rate), 0.0)
            value = value + scaled(coef, pieces[b])
        low_value = value.astype(BF16)
        outs.append(low_value if d == 0 else swap(low_value, "tensor", d))
    bit = 1
    while bit < width:
        flip = (mine & bit) != 0
        outs = [jnp.where(flip, outs[u ^ bit], outs[u]) for u in range(width)]
        bit *= 2
    return jnp.concatenate(outs, axis=1)


def reduce_line(value, axis):
    count = lax.axis_size(axis)
    mine = lax.axis_index(axis)
    bits = []
    bit = 1
    while bit < count:
        bits.append(bit)
        bit *= 2
    for bit in bits:
        which = (mine & bit) // bit
        sent = swap(take_half(value, 1 - which).astype(BF16), axis, bit)
        value = take_half(value, which) + sent.astype(F32)
    value = value.astype(BF16)
    for bit in reversed(bits):
        which = (mine & bit) // bit
        value = join_half(value, swap(value, axis, bit), which)
    return value


def norm_rows(values):
    inv_scale = lax.rsqrt(jnp.mean(values * values, axis=-1, keepdims=True) + EPS)
    return (values * inv_scale, inv_scale)


def norm_back(gradient, normed, inv_scale):
    return inv_scale * (gradient - normed * jnp.mean(gradient * normed, axis=-1, keepdims=True))


def rotate(values, cosine, sine_part):
    half_dim = values.shape[-1] // 2
    first_half = values[..., :half_dim]
    second_half = values[..., half_dim:]
    return jnp.concatenate(
        [
            first_half * cosine - second_half * sine_part,
            second_half * cosine + first_half * sine_part,
        ],
        axis=-1,
    )


def rotate_back(values, cosine, sine_part):
    return rotate(values, cosine, -sine_part)


def split_heads(values, head_count):
    seq_count, group_len, model_width = values.shape
    return values.reshape(seq_count, group_len, head_count, model_width // head_count).transpose(
        0, 2, 1, 3
    )


def join_heads(values):
    seq_count, head_count, group_len, head_dim = values.shape
    return values.transpose(0, 2, 1, 3).reshape(seq_count, group_len, head_count * head_dim)


def dot(spec, first, second):
    return jnp.einsum(spec, first, second, preferred_element_type=F32)


def project(inputs, matrix):
    return dot("scd,de->sce", inputs, matrix)


def project_back(gradient, matrix):
    return dot("sce,de->scd", gradient, matrix)


def weight_grad(inputs, gradient):
    return dot("scd,sce->de", inputs, gradient)


def silu_slope(values):
    sigmoid_v = jax.nn.sigmoid(values)
    return sigmoid_v * (1.0 + values * (1.0 - sigmoid_v))


def on_device(
    tokens,
    w_query,
    w_key,
    w_value,
    w_ugate,
    w_output,
    w_left,
    w_right,
    w_down,
    decay_rate,
    cotangent,
):
    seq_count, group_len, model_width = tokens.shape
    head_count = decay_rate.shape[0]
    head_dim = model_width // head_count
    half_dim = head_dim // 2
    row_count = seq_count * group_len
    core = lax.axis_index("dp")

    shard = (w_left, w_right, w_down)
    fetched = swap(tuple(take_half(w, core) for w in shard), "tensor", 2)
    swapped = swap(fetched, "dp", 1)
    other = tuple(join_half(f, s, core) for f, s in zip(fetched, swapped))
    grad_res = cotangent.astype(F32)
    grad_own = cotangent.reshape(row_count, model_width)
    grad_nb = swap(grad_own, "tensor", 1)

    position_block = lax.axis_index(("seq", "tensor"))
    places = (position_block * group_len + jnp.arange(group_len)).astype(F32)
    frequency = 10000.0 ** (-jnp.arange(half_dim, dtype=F32) / half_dim)
    angles = places[:, None] * frequency[None, :]
    cosine = jnp.cos(angles)
    sine_part = jnp.sin(angles)
    step_pos = jnp.arange(group_len, dtype=F32)
    lag_steps = step_pos[:, None] - step_pos[None, :]
    decay_mask = jnp.where(
        lag_steps >= 0, jnp.exp(-decay_rate[:, None, None] * jnp.maximum(lag_steps, 0.0)), 0.0
    )
    query_weight = jnp.exp(-decay_rate[:, None] * (step_pos + 1.0))[:, :, None]
    key_weight = jnp.exp(-decay_rate[:, None] * (group_len - 1.0 - step_pos))[:, :, None]

    inputs = tokens.astype(F32)
    normed_one, scale_one = norm_rows(inputs)
    normed_low = normed_one.astype(BF16)
    key_pre = project(normed_low, w_key)
    value_pre = project(normed_low, w_value)
    key_rot = rotate(split_heads(jax.nn.silu(key_pre), head_count), cosine, sine_part)
    key_low = key_rot.astype(BF16)
    value_low = split_heads(value_pre, head_count).astype(BF16)
    key_dec = (key_rot * key_weight).astype(BF16)
    local_state = dot("shje,shjf->shef", key_dec, value_low)
    state_low = carried_state(local_state, decay_rate, group_len, False)

    query_pre = project(normed_low, w_query)
    ugate = project(normed_low, w_ugate)
    query_rot = rotate(split_heads(jax.nn.silu(query_pre), head_count), cosine, sine_part)
    query_low = query_rot.astype(BF16)
    query_dec = (query_rot * query_weight).astype(BF16)
    scores = dot("shie,shje->shij", query_low, key_low)
    weights_low = (scores * decay_mask).astype(BF16)
    inner_part = dot("shij,shje->shie", weights_low, value_low)
    outer_part = dot("shie,shef->shif", query_dec, state_low)
    merged = join_heads(inner_part + outer_part)
    normed_att, scale_att = norm_rows(merged)
    gated_low = (normed_att * ugate).astype(BF16)
    residual = inputs + project(gated_low, w_output)
    normed_two, scale_two = norm_rows(residual)
    rows_own = normed_two.astype(BF16).reshape(row_count, model_width)
    rows_nb = swap(rows_own, "tensor", 1)

    def hidden_part(rows, grads):
        mixed = 0.0
        back = 0.0
        kept = []
        for left, right, down in (shard, other):
            e1 = jnp.dot(rows, left, preferred_element_type=F32)
            e2 = jnp.dot(rows, right, preferred_element_type=F32)
            product = (e1 * e2).astype(BF16)
            dm = dot("rd,fd->rf", grads, down)
            de1 = (dm * e2).astype(BF16)
            de2 = (dm * e1).astype(BF16)
            mixed = mixed + jnp.dot(product, down, preferred_element_type=F32)
            back = back + dot("rf,df->rd", de1, left) + dot("rf,df->rd", de2, right)
            kept.append((de1, de2, product))
        return mixed, back, kept

    mixed_nb, back_nb, kept_nb = hidden_part(rows_nb, grad_nb)
    back_in = swap(back_nb.astype(BF16), "tensor", 1)
    mixed_in = swap(mixed_nb.astype(BF16), "tensor", 1)
    mixed_own, back_own, kept_own = hidden_part(rows_own, grad_own)

    shape = (seq_count, group_len, model_width)
    mixed_out = (residual + (mixed_own + mixed_in.astype(F32)).reshape(shape)).astype(BF16)

    rows_all = jnp.concatenate([rows_own, rows_nb], axis=0)
    grads_all = jnp.concatenate([grad_own, grad_nb], axis=0)
    halves = []
    for at in range(2):
        de1, de2, product = (
            jnp.concatenate([first, second], axis=0)
            for first, second in zip(kept_own[at], kept_nb[at])
        )
        full = (
            dot("rd,rf->df", rows_all, de1),
            dot("rd,rf->df", rows_all, de2),
            dot("rf,rd->fd", product, grads_all),
        )
        sent = swap(tuple(take_half(g, 1 - core).astype(BF16) for g in full), "dp", 1)
        halves.append(tuple(take_half(g, core) + s.astype(F32) for g, s in zip(full, sent)))
    from_y = swap(tuple(g.astype(BF16) for g in halves[1]), "tensor", 2)
    hidden_grads = []
    for mine, theirs in zip(halves[0], from_y):
        part = reduce_line(mine + theirs.astype(F32), "seq")
        hidden_grads.append(join_half(part, swap(part, "dp", 1), core).astype(F32))

    grad_normed_two = (back_own + back_in.astype(F32)).reshape(shape)
    grad_mid = grad_res + norm_back(grad_normed_two, normed_two, scale_two)
    grad_branch = grad_mid.astype(BF16)
    grad_gated = project_back(grad_branch, w_output)
    grad_output = weight_grad(gated_low, grad_branch)
    grad_ugate_pre = (grad_gated * normed_att).astype(BF16)
    grad_merged = norm_back(grad_gated * ugate, normed_att, scale_att)
    grad_att = split_heads(grad_merged, head_count).astype(BF16)
    grad_state_in = dot("shie,shif->shef", query_dec, grad_att)
    grad_local_low = carried_state(grad_state_in, decay_rate, group_len, True)

    grad_weights = dot("shie,shje->shij", grad_att, value_low)
    grad_value_heads = dot("shij,shie->shje", weights_low, grad_att)
    grad_scores = (grad_weights * decay_mask).astype(BF16)
    grad_query_rot = dot("shij,shje->shie", grad_scores, key_low)
    grad_key_rot = dot("shij,shie->shje", grad_scores, query_low)
    grad_query_dec = dot("shif,shef->shie", grad_att, state_low)
    grad_query_rot = grad_query_rot + grad_query_dec * query_weight
    grad_query_pre = (
        join_heads(rotate_back(grad_query_rot, cosine, sine_part)) * silu_slope(query_pre)
    ).astype(BF16)
    grad_query = weight_grad(normed_low, grad_query_pre)
    grad_ugate = weight_grad(normed_low, grad_ugate_pre)

    grad_key_dec = dot("shef,shjf->shje", grad_local_low, value_low)
    grad_value_heads = grad_value_heads + dot("shje,shef->shjf", key_dec, grad_local_low)
    grad_key_rot = grad_key_rot + grad_key_dec * key_weight
    grad_key_pre = (
        join_heads(rotate_back(grad_key_rot, cosine, sine_part)) * silu_slope(key_pre)
    ).astype(BF16)
    grad_value_pre = join_heads(grad_value_heads).astype(BF16)
    grad_normed_one = (
        project_back(grad_query_pre, w_query)
        + project_back(grad_key_pre, w_key)
        + project_back(grad_value_pre, w_value)
        + project_back(grad_ugate_pre, w_ugate)
    )
    grad_tokens = grad_mid + norm_back(grad_normed_one, normed_one, scale_one)
    grad_key = weight_grad(normed_low, grad_key_pre)
    grad_value = weight_grad(normed_low, grad_value_pre)

    everyone = ("dp", "seq", "tensor")
    grad_output, grad_ugate = lax.psum(
        (grad_output.astype(BF16), grad_ugate.astype(BF16)), everyone
    )
    grad_query = lax.psum(grad_query.astype(BF16), everyone)
    grad_key, grad_value = lax.psum((grad_key.astype(BF16), grad_value.astype(BF16)), everyone)
    attention_grads = tuple(
        g.astype(F32) for g in (grad_query, grad_key, grad_value, grad_ugate, grad_output)
    )
    return (mixed_out, grad_tokens) + attention_grads + tuple(hidden_grads)


def solution(mesh):
    rows = P("dp", ("seq", "tensor"), None)
    columns = P(None, "tensor")
    return jax.shard_map(
        on_device,
        mesh=mesh,
        in_specs=(rows, P(), P(), P(), P(), P(), columns, columns, P("tensor", None), P(), rows),
        out_specs=(rows, rows, P(), P(), P(), P(), P(), columns, columns, P("tensor", None)),
        check_vma=False,
    )
```

time: 1220 us -> 604 us (0.50)
  waiting for transfers between devices: 879 us -> 303 us
  starting transfers between devices: 1.12 us -> 55.1 us
  blocking collectives: 45.2 us -> 0 us
  local copies, waits for them, and re-layouts: 65.8 us -> 34.2 us
    all_gather x4 -> x0, waiting for transfers between devices: 379 us -> none  [the longest x2 290 us: prefix(): pieces = jax.tree.map(lambda part: lax.all_gather(part, axis), value)]
    psum x2 -> x1, waiting for transfers between devices: 368 us -> 137 us  [on_device(): grad_query = lax.psum(grad_query.astype(BF16), everyone)]
    ppermute x0 -> x52, waiting for transfers between devices: none -> 166 us  [the longest x46 155 us: swap(): lax.ppermute(v, axis, [(i, i ^ bit) for i in range(count)])]
    reduce_scatter x2 -> x0, waiting for transfers between devices: 132 us -> none  [the longest x1 78.4 us: on_device(): lax.psum_scatter(jnp.einsum('rf,df->rd', grad_pair, w_pair, preferred_ele...]
    ppermute x0 -> x52, starting transfers between devices: none -> 55 us  [the longest x46 40.9 us: swap(): lax.ppermute(v, axis, [(i, i ^ bit) for i in range(count)])]
    unnamed x1 -> x0, blocking collectives: 45.2 us -> none
    select_n x30 -> x10, other arithmetic: 45.5 us -> 3.84 us  [the longest x4 2.92 us: carried_state(): outs = [jnp.where(flip, outs[u ^ bit], outs[u]) for u in range(width)]]
    unnamed x135 -> x255, local copies, waits for them, and re-layouts: 45.5 us -> 12.1 us
  transfers between devices with their start and end apart: 8 -> 53, of which waited for: 8 -> 22; matrix products, arithmetic and copies ran while one was open for 12% -> 28% of each run, Pallas kernels for 0% -> 0%
where the time goes in v1:
time: 604 us; the launch traced here: 600 us
  waiting for transfers between devices  303 us (50%)
  matrix products  120 us (20%)
  other arithmetic  72 us (12%)
  starting transfers between devices  55.1 us (9%)
  local copies, waits for them, and re-layouts  34.2 us (6%)
  between operations  16.2 us (3%)
    ppermute x46, waiting for transfers between devices, swap(): lax.ppermute(v, axis, [(i, i ^ bit) for i in range(count)])  155 us
    psum x1, waiting for transfers between devices, on_device(): grad_query = lax.psum(grad_query.astype(BF16), everyone)  137 us
    dot_general x45, matrix products, dot(): return jnp.einsum(spec, first, second, preferred_element_type=F32)  98.3 us
    ppermute x46, starting transfers between devices, swap(): lax.ppermute(v, axis, [(i, i ^ bit) for i in range(count)])  40.9 us
    ppermute x6, starting transfers between devices, shift(): return lax.ppermute(value, axis, pairs)  14.2 us
    convert_element_type x5, other arithmetic, on_device(): g.astype(F32)  14.1 us
  transfers between devices with their start and end apart: 53, of which 22 were waited for; matrix products, arithmetic and copies ran while one was open for 28% of the time, Pallas kernels for 0%

profile of v1, /device:TPU:0, one launch (start us, length us, event | category | flops | bytes accessed | tf_op | source)
XLA Modules:
  0.0 599.7 jit_solution(3760193600378474071)
XLA Ops:
  9.0 4.7 fusion.29
  13.6 2.6 fusion.25
  16.3 3.0 fusion.35
  22.4 3.1 multiply_subtract_fusion.2
  31.9 3.0 collective-permute-start.1
  36.4 2.2 constant_dynamic-slice_fusion.2
  42.6 3.1 fusion.71
  57.5 12.8 %fusion.66 = f32[2,8,256,128]{2,3,1,0:T(8,128)} fusion(bf16[2,8,256,256]{3,2,1,0:T(8,128)(2,1)S(1)} %multiply_convert_fusion.1, bf16[2,8,256,128]{3,1,2,0:T(8,128)(2,1)S(1)} %copy-done.38), kind=kOutput, calls=%fused_computation.148 | convolution fusion | flops 268435456 | bytes 5242880 | tf_op jit(solution)/shard_map/shij,shje->shie/dot_general | solution.py:147
  72.9 6.0 %collective-permute-start.5 = (bf16[2,2,128,128]{3,2,1,0:T(8,128)(2,1)S(1)}, bf16[2,2,128,128]{3,2,1,0:T(8,128)(2,1)S(1)}, u32[]{:S(2)}, u32[]{:S(2)}) collective-permute-start(bf16[2,2,128,128]{3,2,1,0:T(8,128)(2,1)S(1)} %fusion.78), channel_id=1, source_target_pairs={{0,12},{1,13},{2,14},{3,15},{16,28},{17,29},{18,30},{19,31}} | collective-permute-start | bytes 393224 | tf_op jit(solution)/shard_map/ppermute | solution.py:21
  80.3 2.5 collective-permute-start.3
  93.5 2.2 constant_dynamic-slice_fusion
  102.8 2.4 fusion.18
  105.3 2.9 copy.27
  108.2 3.5 multiply_convert_fusion.4
  122.2 20.6 %collective-permute-done.15 = bf16[512,1024]{1,0:T(8,128)(2,1)S(1)} collective-permute-done((bf16[512,1024]{1,0:T(8,128)(2,1)S(1)}, bf16[512,1024]{1,0:T(8,128)(2,1)S(1)}, u32[]{:S(2)}, u32[]{:S(2)}) %collective-permute-start.15) | collective-permute-done | bytes 1048608 | tf_op jit(solution)/shard_map/ppermute | solution.py:14
  144.7 2.2 multiply_convert_fusion.10
  149.0 2.6 fusion.137
  151.5 2.5 fusion.133
  154.0 3.0 multiply_convert_fusion.8
  157.1 2.6 fusion.135
  159.7 2.5 add_convert_fusion.1
  164.8 3.3 add_convert_fusion.3
  168.6 2.3 fusion.134
  171.0 2.3 fusion.138
  173.3 2.3 multiply_convert_fusion.13
  184.4 2.9 fusion.60
  188.3 2.5 fusion.132
  190.8 2.5 fusion.136
  193.3 2.5 fusion.130
  197.5 3.7 fusion.56
  212.7 2.5 multiply_reduce_fusion
  218.3 2.1 fusion.154
  226.6 2.6 fusion.14
  229.8 2.4 collective-permute-start.21
  234.2 2.7 bitcast_convert_fusion
  243.4 2.7 bitcast_convert_fusion.1
  246.1 3.2 collective-permute-done.24
  249.4 5.5 collective-permute-done.23
  260.1 2.3 collective-permute-start.25
  262.4 14.4 %collective-permute-done.38 = bf16[512,704]{0,1:T(8,128)(2,1)S(1)} collective-permute-done((bf16[512,704]{0,1:T(8,128)(2,1)S(1)}, bf16[512,704]{0,1:T(8,128)(2,1)S(1)}, u32[]{:S(2)}, u32[]{:S(2)}) %collective-permute-start.38) | collective-permute-done | bytes 720928 | tf_op jit(solution)/shard_map/ppermute | solution.py:14
  280.4 14.1 %collective-permute-done.26 = bf16[2,2,128,128]{3,2,1,0:T(8,128)(2,1)S(1)} collective-permute-done((bf16[2,2,128,128]{3,2,1,0:T(8,128)(2,1)S(1)}, bf16[2,2,128,128]{3,2,1,0:T(8,128)(2,1)S(1)}, u32[]{:S(2)}, u32[]{:S(2)}) %collective-permute-start.26) | collective-permute-done | bytes 131104 | tf_op jit(solution)/shard_map/ppermute | solution.py:14
  294.5 2.8 collective-permute-start.31
  301.6 2.7 bitcast_convert_fusion.4
  306.5 2.7 bitcast_convert_fusion.3
  309.3 3.0 bitcast_convert_fusion.2
  312.3 2.3 convert_add_fusion.3
  322.1 2.9 collective-permute-start.40
  325.0 10.0 %collective-permute-done.47 = bf16[176,1024]{1,0:T(8,128)(2,1)S(1)} collective-permute-done((bf16[176,1024]{1,0:T(8,128)(2,1)S(1)}, bf16[176,1024]{1,0:T(8,128)(2,1)S(1)}, u32[]{:S(2)}, u32[]{:S(2)}) %collective-permute-start.47) | collective-permute-done | bytes 360480 | tf_op jit(solution)/shard_map/ppermute | solution.py:14
  335.2 5.8 collective-permute-done.32
  341.1 3.4 collective-permute-start.33
  344.5 8.2 %collective-permute-done.40 = bf16[128,704]{0,1:T(8,128)(2,1)S(1)} collective-permute-done((bf16[128,704]{0,1:T(8,128)(2,1)S(1)}, bf16[128,704]{0,1:T(8,128)(2,1)S(1)}, u32[]{:S(2)}, u32[]{:S(2)}) %collective-permute-start.40) | collective-permute-done | bytes 180256 | tf_op jit(solution)/shard_map/ppermute | solution.py:14
  352.8 15.3 %collective-permute-done.48 = bf16[88,1024]{1,0:T(8,128)(2,1)S(1)} collective-permute-done((bf16[88,1024]{1,0:T(8,128)(2,1)S(1)}, bf16[88,1024]{1,0:T(8,128)(2,1)S(1)}, u32[]{:S(2)}, u32[]{:S(2)}) %collective-permute-start.48) | collective-permute-done | bytes 180256 | tf_op jit(solution)/shard_map/ppermute | solution.py:14
  368.3 10.5 %collective-permute-done.33 = bf16[128,704]{0,1:T(8,128)(2,1)S(1)} collective-permute-done((bf16[128,704]{0,1:T(8,128)(2,1)S(1)}, bf16[128,704]{0,1:T(8,128)(2,1)S(1)}, u32[]{:S(2)}, u32[]{:S(2)}) %collective-permute-start.33) | collective-permute-done | bytes 180256 | tf_op jit(solution)/shard_map/ppermute | solution.py:14
  380.6 6.0 collective-permute-done.41
  386.7 7.0 %collective-permute-done.49 = bf16[88,1024]{1,0:T(8,128)(2,1)S(1)} collective-permute-done((bf16[88,1024]{1,0:T(8,128)(2,1)S(1)}, bf16[88,1024]{1,0:T(8,128)(2,1)S(1)}, u32[]{:S(2)}, u32[]{:S(2)}) %collective-permute-start.49) | collective-permute-done | bytes 180256 | tf_op jit(solution)/shard_map/ppermute | solution.py:14
  393.9 9.4 %collective-permute-done.34 = bf16[256,704]{0,1:T(8,128)(2,1)S(1)} collective-permute-done((bf16[256,704]{0,1:T(8,128)(2,1)S(1)}, bf16[256,704]{0,1:T(8,128)(2,1)S(1)}, u32[]{:S(2)}, u32[]{:S(2)}) %collective-permute-start.34) | collective-permute-done | bytes 360480 | tf_op jit(solution)/shard_map/ppermute | solution.py:14
  403.5 15.2 %collective-permute-done.42 = bf16[256,704]{0,1:T(8,128)(2,1)S(1)} collective-permute-done((bf16[256,704]{0,1:T(8,128)(2,1)S(1)}, bf16[256,704]{0,1:T(8,128)(2,1)S(1)}, u32[]{:S(2)}, u32[]{:S(2)}) %collective-permute-start.42) | collective-permute-done | bytes 360480 | tf_op jit(solution)/shard_map/ppermute | solution.py:14
  419.0 14.4 %collective-permute-done.50 = bf16[176,1024]{1,0:T(8,128)(2,1)S(1)} collective-permute-done((bf16[176,1024]{1,0:T(8,128)(2,1)S(1)}, bf16[176,1024]{1,0:T(8,128)(2,1)S(1)}, u32[]{:S(2)}, u32[]{:S(2)}) %collective-permute-start.50) | collective-permute-done | bytes 360480 | tf_op jit(solution)/shard_map/ppermute | solution.py:14
  441.7 136.8 %all-reduce.3.cloned.1.call-done = (bf16[1024,1024]{1,0:T(8,128)(2,1)}, bf16[1024,1024]{1,0:T(8,128)(2,1)}, bf16[1024,1024]{1,0:T(8,128)(2,1)}, bf16[1024,1024]{1,0:T(8,128)(2,1)}, bf16[1024,1024]{1,0:T(8,128)(2,1)}) async-done(((bf16[1024,1024]{1,0:T(8,128)(2,1)}, bf16[1024,1024]{1,0:T(8,128)(2,1)}, bf16[1024,1024]{1,0:T(8,128)(2,1)}, bf16[1024,1024]{1,0:T(8,128)(2,1)}, bf16[1024,1024]{1,0:T(8,128)(2,1)}), ...) | async-done | bytes 10485776 | tf_op jit(solution)/shard_map/psum | solution.py:328
  578.5 4.2 convert_element_type.523
  582.8 2.5 convert_element_type.525
  585.3 2.5 convert_element_type.527
  587.7 2.5 convert_element_type.529
  590.2 2.5 convert_element_type.531
  (446 shorter events, 142.0 us)
Async XLA Ops:
  7.2 104.5 %copy-start = (bf16[1024,1024]{1,0:T(8,128)(2,1)S(1)}, bf16[1024,1024]{1,0:T(8,128)(2,1)}, u32[]{:S(2)}) copy-start(bf16[1024,1024]{1,0:T(8,128)(2,1)} %param.16) | copy-start | bytes 6291460
  7.2 571.4 %all-reduce.3.cloned.1.call-start = ((), (), s32[]{:S(2)}) async-start(), calls=%async_computation | async-start | bytes 20971520 | tf_op jit(solution)/shard_map/psum | solution.py:328
  31.9 39.8 %collective-permute-start.1 = (bf16[2,2,128,128]{3,2,1,0:T(8,128)(2,1)}, bf16[2,2,128,128]{3,2,1,0:T(8,128)(2,1)S(1)}, u32[]{:S(2)}, u32[]{:S(2)}) collective-permute-start(bf16[2,2,128,128]{3,2,1,0:T(8,128)(2,1)} %get-tuple-element.53), channel_id=1, source_target_pairs={{0,2},{1,3},{2,0},{3,1},{4,6},{5,7},{6,4},{7,5},{8,10},{9,11},{10,... | collective-permute-start | bytes 393224 | tf_op jit(solution)/shard_map/ppermute | solution.py:14
  34.9 36.8 %collective-permute-start.2 = (bf16[2,2,128,128]{3,2,1,0:T(8,128)(2,1)}, bf16[2,2,128,128]{3,2,1,0:T(8,128)(2,1)}, u32[]{:S(2)}, u32[]{:S(2)}) collective-permute-start(bf16[2,2,128,128]{3,2,1,0:T(8,128)(2,1)} %get-tuple-element.54), channel_id=1, source_target_pairs={{0,3},{1,2},{2,1},{3,0},{4,7},{5,6},{6,5},{7,4},{8,11},{9,10},{10,... | collective-permute-start | bytes 393224 | tf_op jit(solution)/shard_map/ppermute | solution.py:14
  36.3 35.4 %collective-permute-start = (bf16[2,2,128,128]{3,2,1,0:T(8,128)(2,1)}, bf16[2,2,128,128]{3,2,1,0:T(8,128)(2,1)S(1)}, u32[]{:S(2)}, u32[]{:S(2)}) collective-permute-start(bf16[2,2,128,128]{3,2,1,0:T(8,128)(2,1)} %get-tuple-element.55), channel_id=1, source_target_pairs={{0,1},{1,0},{2,3},{3,2},{4,5},{5,4},{6,7},{7,6},{8,9},{9,8},{10,11... | collective-permute-start | bytes 393224 | tf_op jit(solution)/shard_map/ppermute | solution.py:14
  38.5 83.0 %collective-permute-start.9 = (bf16[512,704]{0,1:T(8,128)(2,1)}, bf16[512,704]{0,1:T(8,128)(2,1)}, u32[]{:S(2)}, u32[]{:S(2)}) collective-permute-start(bf16[512,704]{0,1:T(8,128)(2,1)} %constant_dynamic-slice_fusion.2), channel_id=1, source_target_pairs={{0,2},{1,3},{2,0},{3,1},{4,6},{5,7},{6,4},{7,5},{8,10},{9,11},{10,... | collective-permute-start | bytes 2162696 | tf_op jit(solution)/shard_map/ppermute | solution.py:14
  42.6 79.0 %collective-permute-start.11 = (bf16[512,704]{0,1:T(8,128)(2,1)}, bf16[512,704]{0,1:T(8,128)(2,1)}, u32[]{:S(2)}, u32[]{:S(2)}) collective-permute-start(bf16[512,704]{0,1:T(8,128)(2,1)} %constant_dynamic-slice_fusion.1), channel_id=1, source_target_pairs={{0,2},{1,3},{2,0},{3,1},{4,6},{5,7},{6,4},{7,5},{8,10},{9,11},{10,... | collective-permute-start | bytes 2162696 | tf_op jit(solution)/shard_map/ppermute | solution.py:14
  71.6 21.2 %copy-start.83 = (f32[2]{0:T(128)}, f32[2]{0:T(128)S(1)}, u32[]{:S(2)}) copy-start(f32[2]{0:T(128)S(1)} %get-tuple-element.83) | copy-start | bytes 28
  71.6 21.1 %copy-start.87 = (f32[2]{0:T(128)}, f32[2]{0:T(128)S(1)}, u32[]{:S(2)}) copy-start(f32[2]{0:T(128)S(1)} %get-tuple-element.84) | copy-start | bytes 28
  71.6 21.1 %copy-start.89 = (f32[2]{0:T(128)}, f32[2]{0:T(128)S(1)}, u32[]{:S(2)}) copy-start(f32[2]{0:T(128)S(1)} %get-tuple-element.85) | copy-start | bytes 28
  71.7 21.1 %copy-start.104 = (f32[2]{0:T(128)}, f32[2]{0:T(128)S(1)}, u32[]{:S(2)}) copy-start(f32[2]{0:T(128)S(1)} %get-tuple-element.86) | copy-start | bytes 28
  72.9 11.2 %collective-permute-start.5 = (bf16[2,2,128,128]{3,2,1,0:T(8,128)(2,1)S(1)}, bf16[2,2,128,128]{3,2,1,0:T(8,128)(2,1)S(1)}, u32[]{:S(2)}, u32[]{:S(2)}) collective-permute-start(bf16[2,2,128,128]{3,2,1,0:T(8,128)(2,1)S(1)} %fusion.78), channel_id=1, source_target_pairs={{0,12},{1,13},{2,14},{3,15},{16,28},{17,29},{18,30},{19,31}} | collective-permute-start | bytes 393224 | tf_op jit(solution)/shard_map/ppermute | solution.py:21
  78.9 5.6 collective-permute-start.4
  80.3 5.6 collective-permute-start.3
  88.0 7.7 %collective-permute-start.7 = (bf16[2,2,128,128]{3,2,1,0:T(8,128)(2,1)}, bf16[2,2,128,128]{3,2,1,0:T(8,128)(2,1)}, u32[]{:S(2)}, u32[]{:S(2)}) collective-permute-start(bf16[2,2,128,128]{3,2,1,0:T(8,128)(2,1)} %get-tuple-element.37), channel_id=1, source_target_pairs={{0,2},{1,3},{2,0},{3,1},{4,6},{5,7},{6,4},{7,5},{8,10},{9,11},{10,... | collective-permute-start | bytes 393224 | tf_op jit(solution)/shard_map/ppermute | solution.py:14
  91.3 7.0 %collective-permute-start.6 = (bf16[2,2,128,128]{3,2,1,0:T(8,128)(2,1)}, bf16[2,2,128,128]{3,2,1,0:T(8,128)(2,1)}, u32[]{:S(2)}, u32[]{:S(2)}) collective-permute-start(bf16[2,2,128,128]{3,2,1,0:T(8,128)(2,1)} %fusion.81), channel_id=1, source_target_pairs={{0,3},{1,2},{2,1},{3,0},{4,7},{5,6},{6,5},{7,4},{8,11},{9,10},{10,... | collective-permute-start | bytes 393224 | tf_op jit(solution)/shard_map/ppermute | solution.py:14
  92.9 7.3 %collective-permute-start.8 = (bf16[2,2,128,128]{3,2,1,0:T(8,128)(2,1)}, bf16[2,2,128,128]{3,2,1,0:T(8,128)(2,1)}, u32[]{:S(2)}, u32[]{:S(2)}) collective-permute-start(bf16[2,2,128,128]{3,2,1,0:T(8,128)(2,1)} %get-tuple-element.36), channel_id=1, source_target_pairs={{0,1},{1,0},{2,3},{3,2},{4,5},{5,4},{6,7},{7,6},{8,9},{9,8},{10,11... | collective-permute-start | bytes 393224 | tf_op jit(solution)/shard_map/ppermute | solution.py:14
  95.7 49.1 %collective-permute-start.17 = (bf16[512,1024]{1,0:T(8,128)(2,1)}, bf16[512,1024]{1,0:T(8,128)(2,1)}, u32[]{:S(2)}, u32[]{:S(2)}) collective-permute-start(bf16[512,1024]{1,0:T(8,128)(2,1)} %bitcast.198), channel_id=1, source_target_pairs={{0,1},{1,0},{2,3},{3,2},{4,5},{5,4},{6,7},{7,6},{8,9},{9,8},{10,11... | collective-permute-start | bytes 3145736 | tf_op jit(solution)/shard_map/ppermute | solution.py:14
  98.4 23.8 %collective-permute-start.13 = (bf16[352,1024]{1,0:T(8,128)(2,1)}, bf16[352,1024]{1,0:T(8,128)(2,1)}, u32[]{:S(2)}, u32[]{:S(2)}) collective-permute-start(bf16[352,1024]{1,0:T(8,128)(2,1)} %constant_dynamic-slice_fusion), channel_id=1, source_target_pairs={{0,2},{1,3},{2,0},{3,1},{4,6},{5,7},{6,4},{7,5},{8,10},{9,11},{10,... | collective-permute-start | bytes 2162696 | tf_op jit(solution)/shard_map/ppermute | solution.py:14
  113.3 29.5 %collective-permute-start.15 = (bf16[512,1024]{1,0:T(8,128)(2,1)S(1)}, bf16[512,1024]{1,0:T(8,128)(2,1)S(1)}, u32[]{:S(2)}, u32[]{:S(2)}) collective-permute-start(bf16[512,1024]{1,0:T(8,128)(2,1)S(1)} %bitcast.204), channel_id=1, source_target_pairs={{0,1},{1,0},{2,3},{3,2},{4,5},{5,4},{6,7},{7,6},{8,9},{9,8},{10,11... | collective-permute-start | bytes 3145736 | tf_op jit(solution)/shard_map/ppermute | solution.py:14
  121.5 27.4 %collective-permute-start.10 = (bf16[512,704]{0,1:T(8,128)(2,1)}, bf16[512,704]{0,1:T(8,128)(2,1)S(1)}, u32[]{:S(2)}, u32[]{:S(2)}) collective-permute-start(bf16[512,704]{0,1:T(8,128)(2,1)} %collective-permute-done.9), channel_id=1, source_target_pairs={{0,16},{16,0},{1,17},{17,1},{2,18},{18,2},{3,19},{19,3},{4,20},{20... | collective-permute-start | bytes 2162696 | tf_op jit(solution)/shard_map/ppermute | solution.py:14
  121.6 29.9 %collective-permute-start.12 = (bf16[512,704]{0,1:T(8,128)(2,1)}, bf16[512,704]{0,1:T(8,128)(2,1)S(1)}, u32[]{:S(2)}, u32[]{:S(2)}) collective-permute-start(bf16[512,704]{0,1:T(8,128)(2,1)} %collective-permute-done.11), channel_id=1, source_target_pairs={{0,16},{16,0},{1,17},{17,1},{2,18},{18,2},{3,19},{19,3},{4,20},{20... | collective-permute-start | bytes 2162696 | tf_op jit(solution)/shard_map/ppermute | solution.py:14
  122.1 31.9 %collective-permute-start.14 = (bf16[352,1024]{1,0:T(8,128)(2,1)}, bf16[352,1024]{1,0:T(8,128)(2,1)S(1)}, u32[]{:S(2)}, u32[]{:S(2)}) collective-permute-start(bf16[352,1024]{1,0:T(8,128)(2,1)} %collective-permute-done.13), channel_id=1, source_target_pairs={{0,16},{16,0},{1,17},{17,1},{2,18},{18,2},{3,19},{19,3},{4,20},{20... | collective-permute-start | bytes 2162696 | tf_op jit(solution)/shard_map/ppermute | solution.py:14
  142.8 38.2 %copy-start.119 = (bf16[512,1024]{1,0:T(8,128)(2,1)}, bf16[512,1024]{1,0:T(8,128)(2,1)S(1)}, u32[]{:S(2)}) copy-start(bf16[512,1024]{1,0:T(8,128)(2,1)S(1)} %collective-permute-done.15) | copy-start | bytes 3145732
  149.0 22.0 %copy-start.121 = (bf16[512,704]{0,1:T(8,128)(2,1)}, bf16[512,704]{0,1:T(8,128)(2,1)S(1)}, u32[]{:S(2)}) copy-start(bf16[512,704]{0,1:T(8,128)(2,1)S(1)} %collective-permute-done.10) | copy-start | bytes 2162692
  162.2 46.4 %collective-permute-start.18 = (bf16[512,1024]{1,0:T(8,128)(2,1)S(1)}, bf16[512,1024]{1,0:T(8,128)(2,1)S(1)}, u32[]{:S(2)}, u32[]{:S(2)}) collective-permute-start(bf16[512,1024]{1,0:T(8,128)(2,1)S(1)} %add_convert_fusion.1), channel_id=1, source_target_pairs={{0,1},{1,0},{2,3},{3,2},{4,5},{5,4},{6,7},{7,6},{8,9},{9,8},{10,11... | collective-permute-start | bytes 3145736 | tf_op jit(solution)/shard_map/ppermute | solution.py:14
  168.1 42.2 %collective-permute-start.16 = (bf16[512,1024]{1,0:T(8,128)(2,1)}, bf16[512,1024]{1,0:T(8,128)(2,1)S(1)}, u32[]{:S(2)}, u32[]{:S(2)}) collective-permute-start(bf16[512,1024]{1,0:T(8,128)(2,1)} %add_convert_fusion.3), channel_id=1, source_target_pairs={{0,1},{1,0},{2,3},{3,2},{4,5},{5,4},{6,7},{7,6},{8,9},{9,8},{10,11... | collective-permute-start | bytes 3145736 | tf_op jit(solution)/shard_map/ppermute | solution.py:14
  178.3 25.0 %collective-permute-start.29 = (bf16[512,704]{0,1:T(8,128)(2,1)}, bf16[512,704]{0,1:T(8,128)(2,1)S(1)}, u32[]{:S(2)}, u32[]{:S(2)}) collective-permute-start(bf16[512,704]{0,1:T(8,128)(2,1)} %dynamic-slice_convert_fusion.4), channel_id=1, source_target_pairs={{0,16},{16,0},{1,17},{17,1},{2,18},{18,2},{3,19},{19,3},{4,20},{20... | collective-permute-start | bytes 2162696 | tf_op jit(solution)/shard_map/ppermute | solution.py:14
  183.9 20.9 %collective-permute-start.37 = (bf16[512,704]{0,1:T(8,128)(2,1)}, bf16[512,704]{0,1:T(8,128)(2,1)S(1)}, u32[]{:S(2)}, u32[]{:S(2)}) collective-permute-start(bf16[512,704]{0,1:T(8,128)(2,1)} %dynamic-slice_convert_fusion.2), channel_id=1, source_target_pairs={{0,16},{16,0},{1,17},{17,1},{2,18},{18,2},{3,19},{19,3},{4,20},{20... | collective-permute-start | bytes 2162696 | tf_op jit(solution)/shard_map/ppermute | solution.py:14
  188.3 19.2 %collective-permute-start.45 = (bf16[352,1024]{1,0:T(8,128)(2,1)}, bf16[352,1024]{1,0:T(8,128)(2,1)S(1)}, u32[]{:S(2)}, u32[]{:S(2)}) collective-permute-start(bf16[352,1024]{1,0:T(8,128)(2,1)} %dynamic-slice_convert_fusion), channel_id=1, source_target_pairs={{0,16},{16,0},{1,17},{17,1},{2,18},{18,2},{3,19},{19,3},{4,20},{20... | collective-permute-start | bytes 2162696 | tf_op jit(solution)/shard_map/ppermute | solution.py:14
  203.3 52.8 %collective-permute-start.28 = (bf16[512,704]{0,1:T(8,128)(2,1)}, bf16[512,704]{0,1:T(8,128)(2,1)}, u32[]{:S(2)}, u32[]{:S(2)}) collective-permute-start(bf16[512,704]{0,1:T(8,128)(2,1)} %dynamic-slice_convert_fusion.5), channel_id=1, source_target_pairs={{0,16},{16,0},{1,17},{17,1},{2,18},{18,2},{3,19},{19,3},{4,20},{20... | collective-permute-start | bytes 2162696 | tf_op jit(solution)/shard_map/ppermute | solution.py:14
  204.9 52.9 %collective-permute-start.30 = (bf16[512,704]{0,1:T(8,128)(2,1)}, bf16[512,704]{0,1:T(8,128)(2,1)}, u32[]{:S(2)}, u32[]{:S(2)}) collective-permute-start(bf16[512,704]{0,1:T(8,128)(2,1)} %add_convert_fusion.6), channel_id=1, source_target_pairs={{0,2},{1,3},{2,0},{3,1},{4,6},{5,7},{6,4},{7,5},{8,10},{9,11},{10,... | collective-permute-start | bytes 2162696 | tf_op jit(solution)/shard_map/ppermute | solution.py:14
  229.3 8.1 %collective-permute-start.20 = (bf16[2,2,128,128]{3,2,1,0:T(8,128)(2,1)S(1)}, bf16[2,2,128,128]{3,2,1,0:T(8,128)(2,1)S(1)}, u32[]{:S(2)}, u32[]{:S(2)}) collective-permute-start(bf16[2,2,128,128]{3,2,1,0:T(8,128)(2,1)S(1)} %get-tuple-element.50), channel_id=1, source_target_pairs={{0,2},{1,3},{2,0},{3,1},{4,6},{5,7},{6,4},{7,5},{8,10},{9,11},{10,... | collective-permute-start | bytes 393224 | tf_op jit(solution)/shard_map/ppermute | solution.py:14
  229.8 7.5 %collective-permute-start.21 = (bf16[2,2,128,128]{3,2,1,0:T(8,128)(2,1)S(1)}, bf16[2,2,128,128]{3,2,1,0:T(8,128)(2,1)S(1)}, u32[]{:S(2)}, u32[]{:S(2)}) collective-permute-start(bf16[2,2,128,128]{3,2,1,0:T(8,128)(2,1)S(1)} %get-tuple-element.51), channel_id=1, source_target_pairs={{0,3},{1,2},{2,1},{3,0},{4,7},{5,6},{6,5},{7,4},{8,11},{9,10},{10,... | collective-permute-start | bytes 393224 | tf_op jit(solution)/shard_map/ppermute | solution.py:14
  232.3 6.3 %collective-permute-start.19 = (bf16[2,2,128,128]{3,2,1,0:T(8,128)(2,1)S(1)}, bf16[2,2,128,128]{3,2,1,0:T(8,128)(2,1)S(1)}, u32[]{:S(2)}, u32[]{:S(2)}) collective-permute-start(bf16[2,2,128,128]{3,2,1,0:T(8,128)(2,1)S(1)} %get-tuple-element.52), channel_id=1, source_target_pairs={{0,1},{1,0},{2,3},{3,2},{4,5},{5,4},{6,7},{7,6},{8,9},{9,8},{10,11... | collective-permute-start | bytes 393224 | tf_op jit(solution)/shard_map/ppermute | solution.py:14
  238.9 10.4 %collective-permute-start.24 = (bf16[2,2,128,128]{3,2,1,0:T(8,128)(2,1)S(1)}, bf16[2,2,128,128]{3,2,1,0:T(8,128)(2,1)S(1)}, u32[]{:S(2)}, u32[]{:S(2)}) collective-permute-start(bf16[2,2,128,128]{3,2,1,0:T(8,128)(2,1)S(1)} %fusion.95), channel_id=1, source_target_pairs={{12,0},{13,1},{14,2},{15,3},{28,16},{29,17},{30,18},{31,19}} | collective-permute-start | bytes 393224 | tf_op jit(solution)/shard_map/ppermute | solution.py:21
  240.4 14.5 %collective-permute-start.23 = (bf16[2,2,128,128]{3,2,1,0:T(8,128)(2,1)S(1)}, bf16[2,2,128,128]{3,2,1,0:T(8,128)(2,1)S(1)}, u32[]{:S(2)}, u32[]{:S(2)}) collective-permute-start(bf16[2,2,128,128]{3,2,1,0:T(8,128)(2,1)S(1)} %fusion.95), channel_id=1, source_target_pairs={{8,0},{12,4},{9,1},{13,5},{10,2},{14,6},{11,3},{15,7},{24,16},{28,... | collective-permute-start | bytes 393224 | tf_op jit(solution)/shard_map/ppermute | solution.py:21
  241.7 13.2 %collective-permute-start.22 = (bf16[2,2,128,128]{3,2,1,0:T(8,128)(2,1)S(1)}, bf16[2,2,128,128]{3,2,1,0:T(8,128)(2,1)S(1)}, u32[]{:S(2)}, u32[]{:S(2)}) collective-permute-start(bf16[2,2,128,128]{3,2,1,0:T(8,128)(2,1)S(1)} %fusion.95), channel_id=1, source_target_pairs={{4,0},{8,4},{12,8},{5,1},{9,5},{13,9},{6,2},{10,6},{14,10},{7,3},{... | collective-permute-start | bytes 393224 | tf_op jit(solution)/shard_map/ppermute | solution.py:21
  249.4 10.8 %collective-permute-start.36 = (bf16[512,704]{0,1:T(8,128)(2,1)S(1)}, bf16[512,704]{0,1:T(8,128)(2,1)S(1)}, u32[]{:S(2)}, u32[]{:S(2)}) collective-permute-start(bf16[512,704]{0,1:T(8,128)(2,1)S(1)} %copy-done.67), channel_id=1, source_target_pairs={{0,16},{16,0},{1,17},{17,1},{2,18},{18,2},{3,19},{19,3},{4,20},{20... | collective-permute-start | bytes 2162696 | tf_op jit(solution)/shard_map/ppermute | solution.py:14
  254.9 57.4 %collective-permute-start.44 = (bf16[352,1024]{1,0:T(8,128)(2,1)}, bf16[352,1024]{1,0:T(8,128)(2,1)}, u32[]{:S(2)}, u32[]{:S(2)}) collective-permute-start(bf16[352,1024]{1,0:T(8,128)(2,1)} %dynamic-slice_convert_fusion.1), channel_id=1, source_target_pairs={{0,16},{16,0},{1,17},{17,1},{2,18},{18,2},{3,19},{19,3},{4,20},{20... | collective-permute-start | bytes 2162696 | tf_op jit(solution)/shard_map/ppermute | solution.py:14
  254.9 21.9 %collective-permute-start.38 = (bf16[512,704]{0,1:T(8,128)(2,1)S(1)}, bf16[512,704]{0,1:T(8,128)(2,1)S(1)}, u32[]{:S(2)}, u32[]{:S(2)}) collective-permute-start(bf16[512,704]{0,1:T(8,128)(2,1)S(1)} %copy-done.68), channel_id=1, source_target_pairs={{0,2},{1,3},{2,0},{3,1},{4,6},{5,7},{6,4},{7,5},{8,10},{9,11},{10,... | collective-permute-start | bytes 2162696 | tf_op jit(solution)/shard_map/ppermute | solution.py:14
  256.1 56.2 %collective-permute-start.46 = (bf16[352,1024]{1,0:T(8,128)(2,1)}, bf16[352,1024]{1,0:T(8,128)(2,1)}, u32[]{:S(2)}, u32[]{:S(2)}) collective-permute-start(bf16[352,1024]{1,0:T(8,128)(2,1)} %add_convert_fusion.4), channel_id=1, source_target_pairs={{0,2},{1,3},{2,0},{3,1},{4,6},{5,7},{6,4},{7,5},{8,10},{9,11},{10,... | collective-permute-start | bytes 2162696 | tf_op jit(solution)/shard_map/ppermute | solution.py:14
  257.7 36.8 %collective-permute-start.26 = (bf16[2,2,128,128]{3,2,1,0:T(8,128)(2,1)S(1)}, bf16[2,2,128,128]{3,2,1,0:T(8,128)(2,1)S(1)}, u32[]{:S(2)}, u32[]{:S(2)}) collective-permute-start(bf16[2,2,128,128]{3,2,1,0:T(8,128)(2,1)S(1)} %get-tuple-element.35), channel_id=1, source_target_pairs={{0,2},{1,3},{2,0},{3,1},{4,6},{5,7},{6,4},{7,5},{8,10},{9,11},{10,... | collective-permute-start | bytes 393224 | tf_op jit(solution)/shard_map/ppermute | solution.py:14
  260.1 37.2 %collective-permute-start.25 = (bf16[2,2,128,128]{3,2,1,0:T(8,128)(2,1)S(1)}, bf16[2,2,128,128]{3,2,1,0:T(8,128)(2,1)S(1)}, u32[]{:S(2)}, u32[]{:S(2)}) collective-permute-start(bf16[2,2,128,128]{3,2,1,0:T(8,128)(2,1)S(1)} %fusion.98), channel_id=1, source_target_pairs={{0,3},{1,2},{2,1},{3,0},{4,7},{5,6},{6,5},{7,4},{8,11},{9,10},{10,... | collective-permute-start | bytes 393224 | tf_op jit(solution)/shard_map/ppermute | solution.py:14
  276.8 20.5 %collective-permute-start.27 = (bf16[2,2,128,128]{3,2,1,0:T(8,128)(2,1)S(1)}, bf16[2,2,128,128]{3,2,1,0:T(8,128)(2,1)S(1)}, u32[]{:S(2)}, u32[]{:S(2)}) collective-permute-start(bf16[2,2,128,128]{3,2,1,0:T(8,128)(2,1)S(1)} %get-tuple-element.34), channel_id=1, source_target_pairs={{0,1},{1,0},{2,3},{3,2},{4,5},{5,4},{6,7},{7,6},{8,9},{9,8},{10,11... | collective-permute-start | bytes 393224 | tf_op jit(solution)/shard_map/ppermute | solution.py:14
  294.5 24.9 %collective-permute-start.31 = (bf16[256,704]{0,1:T(8,128)(2,1)}, bf16[256,704]{0,1:T(8,128)(2,1)}, u32[]{:S(2)}, u32[]{:S(2)}) collective-permute-start(bf16[256,704]{0,1:T(8,128)(2,1)} %dynamic-slice_convert_fusion.8), channel_id=1, source_target_pairs={{0,4},{4,0},{8,12},{12,8},{1,5},{5,1},{9,13},{13,9},{2,6},{6,2},{1... | collective-permute-start | bytes 1081352 | tf_op jit(solution)/shard_map/ppermute | solution.py:14
  297.3 23.5 %collective-permute-start.39 = (bf16[256,704]{0,1:T(8,128)(2,1)}, bf16[256,704]{0,1:T(8,128)(2,1)}, u32[]{:S(2)}, u32[]{:S(2)}) collective-permute-start(bf16[256,704]{0,1:T(8,128)(2,1)} %dynamic-slice_convert_fusion.7), channel_id=1, source_target_pairs={{0,4},{4,0},{8,12},{12,8},{1,5},{5,1},{9,13},{13,9},{2,6},{6,2},{1... | collective-permute-start | bytes 1081352 | tf_op jit(solution)/shard_map/ppermute | solution.py:14
  314.7 20.3 %collective-permute-start.47 = (bf16[176,1024]{1,0:T(8,128)(2,1)S(1)}, bf16[176,1024]{1,0:T(8,128)(2,1)S(1)}, u32[]{:S(2)}, u32[]{:S(2)}) collective-permute-start(bf16[176,1024]{1,0:T(8,128)(2,1)S(1)} %dynamic-slice_convert_fusion.6), channel_id=1, source_target_pairs={{0,4},{4,0},{8,12},{12,8},{1,5},{5,1},{9,13},{13,9},{2,6},{6,2},{1... | collective-permute-start | bytes 1081352 | tf_op jit(solution)/shard_map/ppermute | solution.py:14
  320.8 20.2 %collective-permute-start.32 = (bf16[128,704]{0,1:T(8,128)(2,1)S(1)}, bf16[128,704]{0,1:T(8,128)(2,1)S(1)}, u32[]{:S(2)}, u32[]{:S(2)}) collective-permute-start(bf16[128,704]{0,1:T(8,128)(2,1)S(1)} %dynamic-slice_convert_fusion.11), channel_id=1, source_target_pairs={{0,8},{4,12},{8,0},{12,4},{1,9},{5,13},{9,1},{13,5},{2,10},{6,14},... | collective-permute-start | bytes 540680 | tf_op jit(solution)/shard_map/ppermute | solution.py:14
  322.0 57.0 %copy-start.41 = (f32[2,256,1024]{2,1,0:T(8,128)S(1)}, f32[2,256,1024]{2,1,0:T(8,128)}, u32[]{:S(2)}) copy-start(f32[2,256,1024]{2,1,0:T(8,128)} %fusion.14) | copy-start | bytes 6291460
  322.0 57.0 %copy-start.37 = (bf16[2,256,1024]{2,1,0:T(8,128)(2,1)S(1)}, bf16[2,256,1024]{2,1,0:T(8,128)(2,1)}, u32[]{:S(2)}) copy-start(bf16[2,256,1024]{2,1,0:T(8,128)(2,1)} %copy-done.36) | copy-start | bytes 3145732
  322.1 57.0 %copy-start.40 = (bf16[1024,1024]{1,0:T(8,128)(2,1)S(1)}, bf16[1024,1024]{1,0:T(8,128)(2,1)}, u32[]{:S(2)}) copy-start(bf16[1024,1024]{1,0:T(8,128)(2,1)} %param.12) | copy-start | bytes 6291460
  322.1 30.6 %collective-permute-start.40 = (bf16[128,704]{0,1:T(8,128)(2,1)S(1)}, bf16[128,704]{0,1:T(8,128)(2,1)S(1)}, u32[]{:S(2)}, u32[]{:S(2)}) collective-permute-start(bf16[128,704]{0,1:T(8,128)(2,1)S(1)} %dynamic-slice_convert_fusion.10), channel_id=1, source_target_pairs={{0,8},{4,12},{8,0},{12,4},{1,9},{5,13},{9,1},{13,5},{2,10},{6,14},... | collective-permute-start | bytes 540680 | tf_op jit(solution)/shard_map/ppermute | solution.py:14
  335.2 33.0 %collective-permute-start.48 = (bf16[88,1024]{1,0:T(8,128)(2,1)S(1)}, bf16[88,1024]{1,0:T(8,128)(2,1)S(1)}, u32[]{:S(2)}, u32[]{:S(2)}) collective-permute-start(bf16[88,1024]{1,0:T(8,128)(2,1)S(1)} %dynamic-slice_convert_fusion.9), channel_id=1, source_target_pairs={{0,8},{4,12},{8,0},{12,4},{1,9},{5,13},{9,1},{13,5},{2,10},{6,14},... | collective-permute-start | bytes 540680 | tf_op jit(solution)/shard_map/ppermute | solution.py:14
  341.1 37.7 %collective-permute-start.33 = (bf16[128,704]{0,1:T(8,128)(2,1)S(1)}, bf16[128,704]{0,1:T(8,128)(2,1)S(1)}, u32[]{:S(2)}, u32[]{:S(2)}) collective-permute-start(bf16[128,704]{0,1:T(8,128)(2,1)S(1)} %add_convert_fusion.9), channel_id=1, source_target_pairs={{0,8},{4,12},{8,0},{12,4},{1,9},{5,13},{9,1},{13,5},{2,10},{6,14},... | collective-permute-start | bytes 540680 | tf_op jit(solution)/shard_map/ppermute | solution.py:14
  352.7 33.8 %collective-permute-start.41 = (bf16[128,704]{0,1:T(8,128)(2,1)S(1)}, bf16[128,704]{0,1:T(8,128)(2,1)S(1)}, u32[]{:S(2)}, u32[]{:S(2)}) collective-permute-start(bf16[128,704]{0,1:T(8,128)(2,1)S(1)} %add_convert_fusion.8), channel_id=1, source_target_pairs={{0,8},{4,12},{8,0},{12,4},{1,9},{5,13},{9,1},{13,5},{2,10},{6,14},... | collective-permute-start | bytes 540680 | tf_op jit(solution)/shard_map/ppermute | solution.py:14
  368.2 25.6 %collective-permute-start.49 = (bf16[88,1024]{1,0:T(8,128)(2,1)S(1)}, bf16[88,1024]{1,0:T(8,128)(2,1)S(1)}, u32[]{:S(2)}, u32[]{:S(2)}) collective-permute-start(bf16[88,1024]{1,0:T(8,128)(2,1)S(1)} %add_convert_fusion.7), channel_id=1, source_target_pairs={{0,8},{4,12},{8,0},{12,4},{1,9},{5,13},{9,1},{13,5},{2,10},{6,14},... | collective-permute-start | bytes 540680 | tf_op jit(solution)/shard_map/ppermute | solution.py:14
  378.9 24.4 %collective-permute-start.34 = (bf16[256,704]{0,1:T(8,128)(2,1)S(1)}, bf16[256,704]{0,1:T(8,128)(2,1)S(1)}, u32[]{:S(2)}, u32[]{:S(2)}) collective-permute-start(bf16[256,704]{0,1:T(8,128)(2,1)S(1)} %maximum_select_fusion.9), channel_id=1, source_target_pairs={{0,4},{4,0},{8,12},{12,8},{1,5},{5,1},{9,13},{13,9},{2,6},{6,2},{1... | collective-permute-start | bytes 1081352 | tf_op jit(solution)/shard_map/ppermute | solution.py:14
  386.6 32.1 %collective-permute-start.42 = (bf16[256,704]{0,1:T(8,128)(2,1)S(1)}, bf16[256,704]{0,1:T(8,128)(2,1)S(1)}, u32[]{:S(2)}, u32[]{:S(2)}) collective-permute-start(bf16[256,704]{0,1:T(8,128)(2,1)S(1)} %maximum_select_fusion.10), channel_id=1, source_target_pairs={{0,4},{4,0},{8,12},{12,8},{1,5},{5,1},{9,13},{13,9},{2,6},{6,2},{1... | collective-permute-start | bytes 1081352 | tf_op jit(solution)/shard_map/ppermute | solution.py:14
  393.8 39.9 %copy-start.7 = (f32[2,256,1024]{2,1,0:T(8,128)S(1)}, f32[2,256,1024]{2,1,0:T(8,128)}, u32[]{:S(2)}) copy-start(f32[2,256,1024]{2,1,0:T(8,128)} %copy-done.5) | copy-start | bytes 6291460
  393.8 39.6 %collective-permute-start.50 = (bf16[176,1024]{1,0:T(8,128)(2,1)S(1)}, bf16[176,1024]{1,0:T(8,128)(2,1)S(1)}, u32[]{:S(2)}, u32[]{:S(2)}) collective-permute-start(bf16[176,1024]{1,0:T(8,128)(2,1)S(1)} %maximum_select_fusion.11), channel_id=1, source_target_pairs={{0,4},{4,0},{8,12},{12,8},{1,5},{5,1},{9,13},{13,9},{2,6},{6,2},{1... | collective-permute-start | bytes 1081352 | tf_op jit(solution)/shard_map/ppermute | solution.py:14
  403.5 32.2 %collective-permute-start.35 = (bf16[512,704]{0,1:T(8,128)(2,1)S(1)}, bf16[512,704]{0,1:T(8,128)(2,1)S(1)}, u32[]{:S(2)}, u32[]{:S(2)}) collective-permute-start(bf16[512,704]{0,1:T(8,128)(2,1)S(1)} %maximum_select_fusion.6), channel_id=1, source_target_pairs={{0,16},{16,0},{1,17},{17,1},{2,18},{18,2},{3,19},{19,3},{4,20},{20... | collective-permute-start | bytes 2162696 | tf_op jit(solution)/shard_map/ppermute | solution.py:14
  418.9 18.7 %collective-permute-start.43 = (bf16[512,704]{0,1:T(8,128)(2,1)S(1)}, bf16[512,704]{0,1:T(8,128)(2,1)S(1)}, u32[]{:S(2)}, u32[]{:S(2)}) collective-permute-start(bf16[512,704]{0,1:T(8,128)(2,1)S(1)} %maximum_select_fusion.7), channel_id=1, source_target_pairs={{0,16},{16,0},{1,17},{17,1},{2,18},{18,2},{3,19},{19,3},{4,20},{20... | collective-permute-start | bytes 2162696 | tf_op jit(solution)/shard_map/ppermute | solution.py:14
  433.7 5.9 collective-permute-start.51
  (116 other events, 823.7 us)
Sparse Core Ops, SparseCore 0:
  312.4 266.0 all-reduce.2

commit v2 on v1

--- a/solution.py
+++ b/solution.py
@@ -1,6 +1,8 @@
 import jax
 import jax.numpy as jnp
 from jax import lax
+from jax.experimental import pallas as pl
+from jax.experimental.pallas import tpu as pltpu
 from jax.sharding import PartitionSpec as P
 
 EPS = 1e-06
@@ -86,23 +88,407 @@
     return jnp.concatenate(outs, axis=1)
 
 
-def reduce_line(value, axis):
-    count = lax.axis_size(axis)
-    mine = lax.axis_index(axis)
-    bits = []
-    bit = 1
-    while bit < count:
-        bits.append(bit)
-        bit *= 2
-    for bit in bits:
-        which = (mine & bit) // bit
-        sent = swap(take_half(value, 1 - which).astype(BF16), axis, bit)
-        value = take_half(value, which) + sent.astype(F32)
-    value = value.astype(BF16)
-    for bit in reversed(bits):
-        which = (mine & bit) // bit
-        value = join_half(value, swap(value, axis, bit), which)
-    return value
+CHUNK = 256
+LAG = 2
+
+
+def added(first, second):
+    return (first.astype(F32) + second.astype(F32)).astype(BF16)
+
+
+def reduce_kernel(
+    depth,
+    grads,
+    pair_in,
+    down_in,
+    out,
+    pair_out,
+    down_out,
+    own,
+    core_in,
+    first_in,
+    second_in,
+    line_in,
+    line_mid,
+    pair_line,
+    pair_mid,
+    down_line,
+    down_mid,
+    sems,
+    pair_sems,
+    down_sems,
+    load_sem,
+):
+    core = lax.axis_index("dp")
+    slot = lax.axis_index("tensor")
+    place = lax.axis_index("seq")
+    rows = own.shape[0]
+    chunks = rows // CHUNK
+    half, quarter, eighth = CHUNK // 2, CHUNK // 4, CHUNK // 8
+    low_side = place < depth // 2
+    outermost = (place == 0) | (place == depth - 1)
+    middle = (place == depth // 2 - 1) | (place == depth // 2)
+    inward = jnp.where(low_side, place + 1, place - 1)
+    outward = jnp.where(low_side, place - 1, place + 1)
+
+    barrier = pltpu.get_barrier_semaphore()
+
+    def greet(peer):
+        pl.semaphore_signal(
+            barrier, inc=1, device_id=peer, device_id_type=pl.DeviceIdType.MESH
+        )
+
+    greet({"dp": 1 - core})
+    greet({"tensor": slot ^ 1})
+    greet({"tensor": slot ^ 2})
+
+    @pl.when(place > 0)
+    def _():
+        greet({"seq": place - 1})
+
+    @pl.when(place < depth - 1)
+    def _():
+        greet({"seq": place + 1})
+
+    pl.semaphore_wait(barrier, jnp.where(outermost, 4, 5))
+
+    def remote(source, target, sem, at, peer):
+        return pltpu.make_async_remote_copy(
+            src_ref=source,
+            dst_ref=target,
+            send_sem=sem.at[0, at],
+            recv_sem=sem.at[1, at],
+            device_id=peer,
+            device_id_type=pl.DeviceIdType.MESH,
+        )
+
+    def span(start, size):
+        return pl.ds(pl.multiple_of(start, size), size)
+
+    def bits(q):
+        first = jnp.where(q % 2 == 0, 1, 2)
+        second = 3 - first
+        return first, second, (slot & first) // first, (slot & second) // second
+
+    def base(q):
+        return pl.multiple_of(q * CHUNK, CHUNK)
+
+    def to_core(q):
+        return remote(
+            own.at[span(base(q) + (1 - core) * half, half)],
+            core_in.at[q],
+            sems.at[0],
+            q,
+            {"dp": 1 - core},
+        )
+
+    def to_first(q):
+        first, _, f, _ = bits(q)
+        return remote(
+            core_in.at[q, span((1 - f) * quarter, quarter)],
+            first_in.at[q],
+            sems.at[1],
+            q,
+            {"tensor": slot ^ first},
+        )
+
+    def to_second(q):
+        _, second, _, g = bits(q)
+        return remote(
+            first_in.at[q, span((1 - g) * eighth, eighth)],
+            second_in.at[q],
+            sems.at[2],
+            q,
+            {"tensor": slot ^ second},
+        )
+
+    def block(q):
+        _, _, f, g = bits(q)
+        return base(q) + core * half + f * quarter + g * eighth
+
+    def back_second(q):
+        _, second, _, _ = bits(q)
+        at = span(block(q), eighth)
+        return remote(out.at[at], out.at[at], sems.at[3], q, {"tensor": slot ^ second})
+
+    def back_first(q):
+        first, _, f, _ = bits(q)
+        at = span(base(q) + core * half + f * quarter, quarter)
+        return remote(out.at[at], out.at[at], sems.at[4], q, {"tensor": slot ^ first})
+
+    def back_core(q):
+        at = span(base(q) + core * half, half)
+        return remote(out.at[at], out.at[at], sems.at[5], q, {"dp": 1 - core})
+
+    class Line:
+        def __init__(self, mine, came, met, total, sem, offset):
+            self.mine, self.came, self.met, self.total = mine, came, met, total
+            self.sem, self.offset = sem, offset
+
+        def inwards(self, q, source):
+            return remote(
+                source, self.came(q), self.sem.at[self.offset], q, {"seq": inward}
+            )
+
+        def across(self, q):
+            return remote(
+                self.came(q),
+                self.met(q),
+                self.sem.at[self.offset + 1],
+                q,
+                {"seq": depth - 1 - place},
+            )
+
+        def outwards(self, q):
+            return remote(
+                self.total(q), self.total(q), self.sem.at[self.offset + 2], q, {"seq": outward}
+            )
+
+        def step_in(self, q):
+            @pl.when(outermost)
+            def _():
+                self.inwards(q, self.mine(q)).start()
+
+        def step_middle(self, q):
+            @pl.when(jnp.logical_not(outermost))
+            def _():
+                self.inwards(q, self.mine(q)).wait_recv()
+                came = self.came(q)
+                came[...] = added(self.mine(q)[...], came[...])
+
+                @pl.when(middle)
+                def _():
+                    self.across(q).start()
+
+                @pl.when(jnp.logical_not(middle))
+                def _():
+                    self.inwards(q, came).start()
+
+        def step_out(self, q):
+            @pl.when(middle)
+            def _():
+                self.across(q).wait_recv()
+                self.total(q)[...] = added(self.came(q)[...], self.met(q)[...])
+
+            @pl.when(jnp.logical_not(outermost))
+            def _():
+                @pl.when(jnp.logical_not(middle))
+                def _():
+                    self.outwards(q).wait_recv()
+
+                self.outwards(q).start()
+
+        def step_last(self, q):
+            @pl.when(outermost)
+            def _():
+                self.outwards(q).wait_recv()
+
+        def settle(self, q):
+            @pl.when(outermost)
+            def _():
+                self.inwards(q, self.mine(q)).wait_send()
+
+            @pl.when(jnp.logical_not(outermost))
+            def _():
+                @pl.when(middle)
+                def _():
+                    self.across(q).wait_send()
+
+                @pl.when(jnp.logical_not(middle))
+                def _():
+                    self.inwards(q, self.came(q)).wait_send()
+
+                self.outwards(q).wait_send()
+
+    def second_mine(q):
+        return second_in.at[q]
+
+    line = Line(
+        second_mine,
+        lambda q: line_in.at[q],
+        lambda q: line_mid.at[q],
+        lambda q: out.at[span(block(q), eighth)],
+        sems,
+        6,
+    )
+    pair_chunks = pair_line.shape[0]
+    pair_rows = pair_line.shape[1]
+    per_side = pair_chunks // 2
+    pair = Line(
+        lambda q: pair_in.at[span(q * pair_rows, pair_rows)],
+        lambda q: pair_line.at[q],
+        lambda q: pair_mid.at[q],
+        lambda q: pair_out.at[q // per_side, core, span((q % per_side) * pair_rows, pair_rows)],
+        pair_sems,
+        0,
+    )
+    down_chunks = down_line.shape[0]
+    down_rows = down_line.shape[1]
+    down_half = down_line.shape[2]
+    down = Line(
+        lambda q: down_in.at[span(q * down_rows, down_rows)],
+        lambda q: down_line.at[q],
+        lambda q: down_mid.at[q],
+        lambda q: down_out.at[span(q * down_rows, down_rows), span(core * down_half, down_half)],
+        down_sems,
+        0,
+    )
+
+    def pair_core(q):
+        return remote(pair.total(q), pair.total(q), pair_sems.at[3], q, {"dp": 1 - core})
+
+    def down_core(q):
+        return remote(down.total(q), down.total(q), down_sems.at[3], q, {"dp": 1 - core})
+
+    size = rows // len(grads)
+    loads = [
+        pltpu.make_async_copy(g, own.at[pl.ds(i * size, size)], load_sem.at[i])
+        for i, g in enumerate(grads)
+    ]
+    for load in loads:
+        load.start()
+    per_load = size // CHUNK
+    for i, load in enumerate(loads):
+        load.wait()
+
+        @pl.loop(i * per_load, (i + 1) * per_load)
+        def _(q):
+            to_core(q).start()
+
+    def stage_a(q):
+        to_core(q).wait_recv()
+        came = core_in.at[q]
+        came[...] = added(own[span(base(q) + core * half, half)], came[...])
+
+    def stage_b(q):
+        _, _, f, _ = bits(q)
+        to_first(q).wait_recv()
+        came = first_in.at[q]
+        came[...] = added(core_in[q, span(f * quarter, quarter)], came[...])
+
+    def stage_c(q):
+        _, _, _, g = bits(q)
+        to_second(q).wait_recv()
+        came = second_in.at[q]
+        came[...] = added(first_in[q, span(g * eighth, eighth)], came[...])
+
+    pairs = chunks // 2
+
+    def during(step, lag, count, action):
+        i = step - lag
+
+        @pl.when((i >= 0) & (i < count))
+        def _():
+            action(i)
+
+    def both(action):
+        def run(i):
+            action(2 * i)
+            action(2 * i + 1)
+
+        return run
+
+    def start(copy):
+        return lambda q: copy(q).start()
+
+    def arrived(copy, following):
+        def run(q):
+            copy(q).wait_recv()
+            following(q).start()
+
+        return run
+
+    def last_then_second(q):
+        line.step_last(q)
+        back_second(q).start()
+
+    steps = max(pairs + 7 * LAG, pair_chunks + down_chunks + 4 * LAG) + 1
+
+    @pl.loop(0, steps)
+    def _(step):
+        during(step, 7 * LAG, pairs, both(arrived(back_first, back_core)))
+        during(step, 6 * LAG, pairs, both(arrived(back_second, back_first)))
+        during(step, 5 * LAG, pairs, both(last_then_second))
+        during(step, 4 * LAG, pairs, both(line.step_out))
+        during(step, 3 * LAG, pairs, both(line.step_middle))
+        during(step, 2 * LAG, pairs, both(stage_c))
+        during(step, LAG, pairs, both(stage_b))
+        during(step, 0, pairs, both(stage_a))
+        during(step, 2 * LAG, pairs, both(line.step_in))
+        during(step, LAG, pairs, both(start(to_second)))
+        during(step, 0, pairs, both(start(to_first)))
+        for stream, count, late, send in (
+            (pair, pair_chunks, 0, pair_core),
+            (down, down_chunks, pair_chunks, down_core),
+        ):
+            def finish(q, stream=stream, send=send):
+                stream.step_last(q)
+                send(q).start()
+
+            during(step, late + 3 * LAG, count, finish)
+            during(step, late + 2 * LAG, count, stream.step_out)
+            during(step, late + LAG, count, stream.step_middle)
+            during(step, late, count, stream.step_in)
+
+    @pl.loop(0, chunks)
+    def _(q):
+        back_core(q).wait_recv()
+        for copy in (to_core, to_first, to_second, back_second, back_first, back_core):
+            copy(q).wait_send()
+        line.settle(q)
+
+    for stream, count, send in ((pair, pair_chunks, pair_core), (down, down_chunks, down_core)):
+
+        @pl.loop(0, count)
+        def _(q, stream=stream, send=send):
+            send(q).wait()
+            stream.settle(q)
+
+
+def reduce_grads(grads, pair_half, down_half, depth):
+    size, width = grads[0].shape
+    rows = size * len(grads)
+    chunks = rows // CHUNK
+    hidden = pair_half.shape[1]
+    pair_chunks, down_chunks = 8, 4
+    pair_rows = pair_half.shape[0] // pair_chunks
+    down_rows = down_half.shape[0] // down_chunks
+    down_cols = down_half.shape[1]
+    vmem = pl.BlockSpec(memory_space=pltpu.VMEM)
+
+    def body(*refs):
+        reduce_kernel(depth, refs[: len(grads)], *refs[len(grads) :])
+
+    return pl.pallas_call(
+        body,
+        out_shape=(
+            jax.ShapeDtypeStruct((rows, width), BF16),
+            jax.ShapeDtypeStruct((2, 2, pair_half.shape[0] // 2, hidden), BF16),
+            jax.ShapeDtypeStruct((down_half.shape[0], 2 * down_cols), BF16),
+        ),
+        in_specs=[pl.BlockSpec(memory_space=pl.ANY)] * len(grads) + [vmem, vmem],
+        out_specs=(vmem, vmem, vmem),
+        scratch_shapes=[
+            pltpu.VMEM((rows, width), BF16),
+            pltpu.VMEM((chunks, CHUNK // 2, width), BF16),
+            pltpu.VMEM((chunks, CHUNK // 4, width), BF16),
+            pltpu.VMEM((chunks, CHUNK // 8, width), BF16),
+            pltpu.VMEM((chunks, CHUNK // 8, width), BF16),
+            pltpu.VMEM((chunks, CHUNK // 8, width), BF16),
+            pltpu.VMEM((pair_chunks, pair_rows, hidden), BF16),
+            pltpu.VMEM((pair_chunks, pair_rows, hidden), BF16),
+            pltpu.VMEM((down_chunks, down_rows, down_cols), BF16),
+            pltpu.VMEM((down_chunks, down_rows, down_cols), BF16),
+            pltpu.SemaphoreType.DMA((9, 2, chunks)),
+            pltpu.SemaphoreType.DMA((4, 2, pair_chunks)),
+            pltpu.SemaphoreType.DMA((4, 2, down_chunks)),
+            pltpu.SemaphoreType.DMA((len(grads),)),
+        ],
+        compiler_params=pltpu.CompilerParams(
+            collective_id=1, has_side_effects=True, vmem_limit_bytes=60 * 1024 * 1024
+        ),
+        name="reduce_grads",
+    )(*grads, pair_half, down_half)
 
 
 def norm_rows(values):
@@ -268,17 +654,20 @@
             for first, second in zip(kept_own[at], kept_nb[at])
         )
         full = (
-            dot("rd,rf->df", rows_all, de1),
-            dot("rd,rf->df", rows_all, de2),
-            dot("rf,rd->fd", product, grads_all),
-        )
-        sent = swap(tuple(take_half(g, 1 - core).astype(BF16) for g in full), "dp", 1)
-        halves.append(tuple(take_half(g, core) + s.astype(F32) for g, s in zip(full, sent)))
+            (dot("rd,rf->df", rows_all, de1), 0),
+            (dot("rd,rf->df", rows_all, de2), 0),
+            (dot("rf,rd->fd", product, grads_all), 1),
+        )
+        sent = swap(
+            tuple(take_half(g, 1 - core, axis).astype(BF16) for g, axis in full), "dp", 1
+        )
+        halves.append(
+            tuple(take_half(g, core, axis) + s.astype(F32) for (g, axis), s in zip(full, sent))
+        )
     from_y = swap(tuple(g.astype(BF16) for g in halves[1]), "tensor", 2)
-    hidden_grads = []
-    for mine, theirs in zip(halves[0], from_y):
-        part = reduce_line(mine + theirs.astype(F32), "seq")
-        hidden_grads.append(join_half(part, swap(part, "dp", 1), core).astype(F32))
+    left_half, right_half, down_half = (
+        added(mine, theirs) for mine, theirs in zip(halves[0], from_y)
+    )
 
     grad_normed_two = (back_own + back_in.astype(F32)).reshape(shape)
     grad_mid = grad_res + norm_back(grad_normed_two, normed_two, scale_two)
@@ -321,16 +710,19 @@
     grad_key = weight_grad(normed_low, grad_key_pre)
     grad_value = weight_grad(normed_low, grad_value_pre)
 
-    everyone = ("dp", "seq", "tensor")
-    grad_output, grad_ugate = lax.psum(
-        (grad_output.astype(BF16), grad_ugate.astype(BF16)), everyone
-    )
-    grad_query = lax.psum(grad_query.astype(BF16), everyone)
-    grad_key, grad_value = lax.psum((grad_key.astype(BF16), grad_value.astype(BF16)), everyone)
+    partial = (grad_query, grad_key, grad_value, grad_ugate, grad_output)
+    sums, pair_sums, down_sums = reduce_grads(
+        tuple(g.astype(BF16) for g in partial),
+        jnp.concatenate([left_half, right_half], axis=0),
+        down_half,
+        lax.axis_size("seq"),
+    )
     attention_grads = tuple(
-        g.astype(F32) for g in (grad_query, grad_key, grad_value, grad_ugate, grad_output)
-    )
-    return (mixed_out, grad_tokens) + attention_grads + tuple(hidden_grads)
+        sums[i * model_width : (i + 1) * model_width].astype(F32) for i in range(len(partial))
+    )
+    pair_sums = pair_sums.reshape(2, model_width, -1).astype(F32)
+    hidden_grads = (pair_sums[0], pair_sums[1], down_sums.astype(F32))
+    return (mixed_out, grad_tokens) + attention_grads + hidden_grads
 
 
 def solution(mesh):

time: 604 us -> 501 us (0.83)
  waiting for transfers between devices: 303 us -> 45.1 us
  Pallas kernels: 0 us -> 124 us
  local copies, waits for them, and re-layouts: 34.2 us -> 67.3 us
  matrix products: 120 us -> 141 us
  between operations: 16.2 us -> 2.63 us
  starting transfers between devices: 55.1 us -> 42.1 us
    psum x1 -> x0, waiting for transfers between devices: 137 us -> none  [on_device(): grad_query = lax.psum(grad_query.astype(BF16), everyone)]
    pallas_call x0 -> x1, Pallas kernels: none -> 124 us  [reduce_grads(): pl.pallas_call(body, out_shape=(jax.ShapeDtypeStruct((rows, width), BF16)...]
    ppermute x46 -> x31, waiting for transfers between devices: 155 us -> 33.9 us  [swap(): lax.ppermute(v, axis, [(i, i ^ bit) for i in range(count)])]
    unnamed x255 -> x319, local copies, waits for them, and re-layouts: 12.1 us -> 30.6 us
    dot_general x45, matrix products: 98.3 us -> 115 us  [dot(): return jnp.einsum(spec, first, second, preferred_element_type=F32)]
    ppermute x46 -> x31, starting transfers between devices: 40.9 us -> 28.1 us  [swap(): lax.ppermute(v, axis, [(i, i ^ bit) for i in range(count)])]
    add x6 -> x0, other arithmetic: 6.82 us -> none  [the longest x3 4.45 us: on_device(): part = reduce_line(mine + theirs.astype(F32), 'seq')]
    convert_element_type x12 -> x8, local copies, waits for them, and re-layouts: 8.18 us -> 12.7 us  [the longest x6 7.56 us: on_device(): take_half(g, 1 - core, axis).astype(BF16)]
  transfers between devices with their start and end apart: 53 -> 37, of which waited for: 22 -> 11; matrix products, arithmetic and copies ran while one was open for 28% -> 38% of each run, Pallas kernels for 0% -> 0%
where the time goes in v2:
time: 501 us; the launch traced here: 496 us
  matrix products  141 us (28%)
  Pallas kernels  124 us (25%)
  other arithmetic  74.1 us (15%)
  local copies, waits for them, and re-layouts  67.3 us (13%)
  waiting for transfers between devices  45.1 us (9%)
  starting transfers between devices  42.1 us (8%)
    pallas_call x1, Pallas kernels, reduce_grads(): pl.pallas_call(body, out_shape=(jax.ShapeDtypeStruct((rows, width), BF16)...  124 us
    dot_general x45, matrix products, dot(): return jnp.einsum(spec, first, second, preferred_element_type=F32)  115 us
    ppermute x31, waiting for transfers between devices, swap(): lax.ppermute(v, axis, [(i, i ^ bit) for i in range(count)])  33.9 us
    unnamed x319, local copies, waits for them, and re-layouts  30.6 us
    ppermute x31, starting transfers between devices, swap(): lax.ppermute(v, axis, [(i, i ^ bit) for i in range(count)])  28.1 us
    ppermute x6, starting transfers between devices, shift(): return lax.ppermute(value, axis, pairs)  14 us
    dot_general x4, matrix products, hidden_part(): mixed = mixed + jnp.dot(product, down, preferred_element_type=F32)  12 us
    ppermute x6, waiting for transfers between devices, shift(): return lax.ppermute(value, axis, pairs)  11.2 us
  transfers between devices with their start and end apart: 37, of which 11 were waited for; matrix products, arithmetic and copies ran while one was open for 38% of the time, Pallas kernels for 0%

profile of v2, /device:TPU:0, one launch (start us, length us, event | category | flops | bytes accessed | tf_op | source)
XLA Modules:
  0.0 496.2 jit_solution(17869188540218467148)
XLA Ops:
  2.4 4.7 fusion.29
  7.1 2.6 fusion.25
  9.7 3.0 fusion.35
  15.8 3.1 multiply_subtract_fusion.2
  25.3 3.0 collective-permute-start.1
  29.8 2.2 constant_dynamic-slice_fusion.4
  36.0 3.1 fusion.68
  51.1 12.8 %fusion.63 = f32[2,8,256,128]{2,3,1,0:T(8,128)} fusion(bf16[2,8,256,256]{3,2,1,0:T(8,128)(2,1)S(1)} %multiply_convert_fusion.1, bf16[2,8,256,128]{3,1,2,0:T(8,128)(2,1)S(1)} %copy-done.43), kind=kOutput, calls=%fused_computation.148 | convolution fusion | flops 268435456 | bytes 5242880 | tf_op jit(solution)/shard_map/shij,shje->shie/dot_general | solution.py:533
  65.3 6.0 %collective-permute-start.5 = (bf16[2,2,128,128]{3,2,1,0:T(8,128)(2,1)S(1)}, bf16[2,2,128,128]{3,2,1,0:T(8,128)(2,1)S(1)}, u32[]{:S(2)}, u32[]{:S(2)}) collective-permute-start(bf16[2,2,128,128]{3,2,1,0:T(8,128)(2,1)S(1)} %fusion.75), channel_id=1, source_target_pairs={{0,12},{1,13},{2,14},{3,15},{16,28},{17,29},{18,30},{19,31}} | collective-permute-start | bytes 393224 | tf_op jit(solution)/shard_map/ppermute | solution.py:23
  72.7 2.5 collective-permute-start.3
  95.3 2.4 fusion.18
  97.7 2.9 copy.101
  100.6 4.8 multiply_convert_fusion.4
  112.9 2.3 fusion.145
  115.2 2.5 fusion.146
  117.7 2.4 fusion.141
  120.7 14.5 %collective-permute-done.15 = bf16[512,1024]{1,0:T(8,128)(2,1)S(1)} collective-permute-done((bf16[512,1024]{1,0:T(8,128)(2,1)S(1)}, bf16[512,1024]{1,0:T(8,128)(2,1)S(1)}, u32[]{:S(2)}, u32[]{:S(2)}) %collective-permute-start.15) | collective-permute-done | bytes 1048608 | tf_op jit(solution)/shard_map/ppermute | solution.py:16
  141.4 2.9 fusion.134
  144.4 2.5 fusion.130
  147.0 3.9 multiply_convert_fusion.8
  150.8 2.6 fusion.132
  153.4 3.4 add_convert_fusion.1
  158.3 2.3 fusion.144
  164.5 2.3 fusion.131
  166.8 2.3 fusion.135
  169.1 3.5 multiply_convert_fusion.13
  176.9 3.0 copy.156
  180.4 3.8 fusion.42
  189.9 3.0 copy.155
  193.0 3.4 fusion.58
  197.1 3.7 fusion.129
  200.9 3.9 fusion.133
  204.8 3.4 add_convert_fusion.3
  208.2 3.8 fusion.127
  212.0 2.9 fusion.54
  214.9 3.4 dynamic-slice_convert_fusion.5
  219.4 2.4 add_convert_fusion.8
  222.3 2.2 add_convert_fusion.9
  227.6 2.5 copy.127
  230.2 2.6 copy.124
  232.8 5.0 %convert_add_fusion.1 = f32[512,1024]{1,0:T(8,128)S(1)} fusion(bf16[512,1024]{1,0:T(8,128)(2,1)} %collective-permute-done.18, f32[512,1024]{1,0:T(8,128)} %fusion.129, f32[512,1024]{1,0:T(8,128)} %fusion.133, f32[512,1024]{1,0:T(8,128)} %fusion.145, f32[512,1024]{1,0:T(8,128)} %fusion.146), kind=kLoop, calls=%fused_computation.70 | loop fusion | flops 2621440 | bytes 11534336 | tf_op jit(solution)/shard_map/add | solution.py:672
  238.2 9.3 %collective-permute-done.16 = bf16[512,1024]{1,0:T(8,128)(2,1)} collective-permute-done((bf16[512,1024]{1,0:T(8,128)(2,1)}, bf16[512,1024]{1,0:T(8,128)(2,1)}, u32[]{:S(2)}, u32[]{:S(2)}) %collective-permute-start.16) | collective-permute-done | bytes 1048608 | tf_op jit(solution)/shard_map/ppermute | solution.py:16
  252.1 2.5 multiply_reduce_fusion
  257.4 3.4 fusion.152
  267.5 2.6 fusion.14
  275.9 2.6 bitcast_convert_fusion.refs_4_
  283.8 2.7 bitcast_convert_fusion.1.refs_3_
  286.5 3.5 collective-permute-done.24
  290.1 5.3 %collective-permute-done.23 = bf16[2,2,128,128]{3,2,1,0:T(8,128)(2,1)S(1)} collective-permute-done((bf16[2,2,128,128]{3,2,1,0:T(8,128)(2,1)S(1)}, bf16[2,2,128,128]{3,2,1,0:T(8,128)(2,1)S(1)}, u32[]{:S(2)}, u32[]{:S(2)}) %collective-permute-start.23) | collective-permute-done | bytes 131104 | tf_op jit(solution)/shard_map/ppermute | solution.py:23
  301.0 2.3 copy.128
  304.8 2.3 copy.125
  307.0 2.5 add_convert_fusion.4
  310.6 6.8 %collective-permute-done.36 = bf16[704,512]{1,0:T(8,128)(2,1)} collective-permute-done((bf16[704,512]{1,0:T(8,128)(2,1)}, bf16[704,512]{1,0:T(8,128)(2,1)}, u32[]{:S(2)}, u32[]{:S(2)}) %collective-permute-start.36) | collective-permute-done | bytes 720928 | tf_op jit(solution)/shard_map/ppermute | solution.py:16
  317.5 2.7 add_convert_fusion.6.refs_6_
  330.5 2.7 bitcast_convert_fusion.3.refs_1_
  336.1 3.0 bitcast_convert_fusion.2.refs_2_
  340.2 2.7 bitcast_convert_fusion.4.refs_0_
  342.9 2.9 fusion.3
  345.8 124.1 %reduce_grads.1 = (bf16[5120,1024]{1,0:T(8,128)(2,1)}, bf16[2,2,512,704]{3,2,1,0:T(8,128)(2,1)}, bf16[704,1024]{1,0:T(8,128)(2,1)}) custom-call(bf16[1024,1024]{1,0:T(8,128)(2,1)} %bitcast_convert_fusion.4.refs_0_, bf16[1024,1024]{1,0:T(8,128)(2,1)} %bitcast_convert_fusion.3.refs_1_, bf16[1024,1024]{1,0:T(8,128)(2,1)} %bitcast_convert_fusion.2.refs_2_, ...), custom_call_target="tpu_custom_call" | custom-call | tf_op jit(solution)/shard_map/reduce_grads/pallas_call | solution.py:462
  469.9 10.7 %slice_convert_fusion = (f32[1024,1024]{1,0:T(8,128)}, f32[1024,1024]{1,0:T(8,128)}, f32[1024,1024]{1,0:T(8,128)}, f32[1024,1024]{1,0:T(8,128)}, f32[1024,1024]{1,0:T(8,128)}) fusion(bf16[5120,1024]{1,0:T(8,128)(2,1)} %get-tuple-element.13), kind=kLoop, calls=%fused_computation.52 | loop fusion | flops 5242880 | bytes 31457280 | tf_op jit(solution)/shard_map/convert_element_type | solution.py:721
  480.6 3.2 fusion.138
  483.8 3.4 copy.129
  487.3 3.4 copy.130
  490.7 3.5 convert_element_type.516
  (462 shorter events, 135.6 us)
Async XLA Ops:
  0.6 104.8 %copy-start = (bf16[1024,1024]{1,0:T(8,128)(2,1)S(1)}, bf16[1024,1024]{1,0:T(8,128)(2,1)}, u32[]{:S(2)}) copy-start(bf16[1024,1024]{1,0:T(8,128)(2,1)} %param.16) | copy-start | bytes 6291460
  25.3 38.8 %collective-permute-start.1 = (bf16[2,2,128,128]{3,2,1,0:T(8,128)(2,1)}, bf16[2,2,128,128]{3,2,1,0:T(8,128)(2,1)S(1)}, u32[]{:S(2)}, u32[]{:S(2)}) collective-permute-start(bf16[2,2,128,128]{3,2,1,0:T(8,128)(2,1)} %get-tuple-element.91), channel_id=1, source_target_pairs={{0,2},{1,3},{2,0},{3,1},{4,6},{5,7},{6,4},{7,5},{8,10},{9,11},{10,... | collective-permute-start | bytes 393224 | tf_op jit(solution)/shard_map/ppermute | solution.py:16
  28.3 35.8 %collective-permute-start.2 = (bf16[2,2,128,128]{3,2,1,0:T(8,128)(2,1)}, bf16[2,2,128,128]{3,2,1,0:T(8,128)(2,1)}, u32[]{:S(2)}, u32[]{:S(2)}) collective-permute-start(bf16[2,2,128,128]{3,2,1,0:T(8,128)(2,1)} %get-tuple-element.92), channel_id=1, source_target_pairs={{0,3},{1,2},{2,1},{3,0},{4,7},{5,6},{6,5},{7,4},{8,11},{9,10},{10,... | collective-permute-start | bytes 393224 | tf_op jit(solution)/shard_map/ppermute | solution.py:16
  29.7 34.4 %collective-permute-start = (bf16[2,2,128,128]{3,2,1,0:T(8,128)(2,1)}, bf16[2,2,128,128]{3,2,1,0:T(8,128)(2,1)S(1)}, u32[]{:S(2)}, u32[]{:S(2)}) collective-permute-start(bf16[2,2,128,128]{3,2,1,0:T(8,128)(2,1)} %get-tuple-element.93), channel_id=1, source_target_pairs={{0,1},{1,0},{2,3},{3,2},{4,5},{5,4},{6,7},{7,6},{8,9},{9,8},{10,11... | collective-permute-start | bytes 393224 | tf_op jit(solution)/shard_map/ppermute | solution.py:16
  32.0 88.2 %collective-permute-start.9 = (bf16[512,704]{0,1:T(8,128)(2,1)}, bf16[512,704]{0,1:T(8,128)(2,1)}, u32[]{:S(2)}, u32[]{:S(2)}) collective-permute-start(bf16[512,704]{0,1:T(8,128)(2,1)} %constant_dynamic-slice_fusion.4), channel_id=1, source_target_pairs={{0,2},{1,3},{2,0},{3,1},{4,6},{5,7},{6,4},{7,5},{8,10},{9,11},{10,... | collective-permute-start | bytes 2162696 | tf_op jit(solution)/shard_map/ppermute | solution.py:16
  36.0 84.2 %collective-permute-start.11 = (bf16[512,704]{0,1:T(8,128)(2,1)}, bf16[512,704]{0,1:T(8,128)(2,1)}, u32[]{:S(2)}, u32[]{:S(2)}) collective-permute-start(bf16[512,704]{0,1:T(8,128)(2,1)} %constant_dynamic-slice_fusion.3), channel_id=1, source_target_pairs={{0,2},{1,3},{2,0},{3,1},{4,6},{5,7},{6,4},{7,5},{8,10},{9,11},{10,... | collective-permute-start | bytes 2162696 | tf_op jit(solution)/shard_map/ppermute | solution.py:16
  64.0 21.2 %copy-start.125 = (f32[2]{0:T(128)}, f32[2]{0:T(128)S(1)}, u32[]{:S(2)}) copy-start(f32[2]{0:T(128)S(1)} %get-tuple-element.52) | copy-start | bytes 28
  64.0 21.1 %copy-start.107 = (f32[2]{0:T(128)}, f32[2]{0:T(128)S(1)}, u32[]{:S(2)}) copy-start(f32[2]{0:T(128)S(1)} %get-tuple-element.121) | copy-start | bytes 28
  64.0 21.1 %copy-start.111 = (f32[2]{0:T(128)}, f32[2]{0:T(128)S(1)}, u32[]{:S(2)}) copy-start(f32[2]{0:T(128)S(1)} %get-tuple-element.122) | copy-start | bytes 28
  64.1 21.1 %copy-start.113 = (f32[2]{0:T(128)}, f32[2]{0:T(128)S(1)}, u32[]{:S(2)}) copy-start(f32[2]{0:T(128)S(1)} %get-tuple-element.123) | copy-start | bytes 28
  64.1 21.1 %copy-start.129 = (f32[2]{0:T(128)}, f32[2]{0:T(128)S(1)}, u32[]{:S(2)}) copy-start(f32[2]{0:T(128)S(1)} %get-tuple-element.124) | copy-start | bytes 28
  64.1 21.1 %copy-start.136 = (f32[2]{0:T(128)}, f32[2]{0:T(128)S(1)}, u32[]{:S(2)}) copy-start(f32[2]{0:T(128)S(1)} %get-tuple-element.120) | copy-start | bytes 28
  65.3 10.5 %collective-permute-start.5 = (bf16[2,2,128,128]{3,2,1,0:T(8,128)(2,1)S(1)}, bf16[2,2,128,128]{3,2,1,0:T(8,128)(2,1)S(1)}, u32[]{:S(2)}, u32[]{:S(2)}) collective-permute-start(bf16[2,2,128,128]{3,2,1,0:T(8,128)(2,1)S(1)} %fusion.75), channel_id=1, source_target_pairs={{0,12},{1,13},{2,14},{3,15},{16,28},{17,29},{18,30},{19,31}} | collective-permute-start | bytes 393224 | tf_op jit(solution)/shard_map/ppermute | solution.py:23
  71.3 5.6 %collective-permute-start.4 = (bf16[2,2,128,128]{3,2,1,0:T(8,128)(2,1)S(1)}, bf16[2,2,128,128]{3,2,1,0:T(8,128)(2,1)S(1)}, u32[]{:S(2)}, u32[]{:S(2)}) collective-permute-start(bf16[2,2,128,128]{3,2,1,0:T(8,128)(2,1)S(1)} %fusion.75), channel_id=1, source_target_pairs={{0,8},{4,12},{1,9},{5,13},{2,10},{6,14},{3,11},{7,15},{16,24},{20,... | collective-permute-start | bytes 393224 | tf_op jit(solution)/shard_map/ppermute | solution.py:23
  72.7 5.6 %collective-permute-start.3 = (bf16[2,2,128,128]{3,2,1,0:T(8,128)(2,1)S(1)}, bf16[2,2,128,128]{3,2,1,0:T(8,128)(2,1)S(1)}, u32[]{:S(2)}, u32[]{:S(2)}) collective-permute-start(bf16[2,2,128,128]{3,2,1,0:T(8,128)(2,1)S(1)} %fusion.75), channel_id=1, source_target_pairs={{0,4},{4,8},{8,12},{1,5},{5,9},{9,13},{2,6},{6,10},{10,14},{3,7},{... | collective-permute-start | bytes 393224 | tf_op jit(solution)/shard_map/ppermute | solution.py:23
  80.4 7.7 %collective-permute-start.7 = (bf16[2,2,128,128]{3,2,1,0:T(8,128)(2,1)}, bf16[2,2,128,128]{3,2,1,0:T(8,128)(2,1)}, u32[]{:S(2)}, u32[]{:S(2)}) collective-permute-start(bf16[2,2,128,128]{3,2,1,0:T(8,128)(2,1)} %get-tuple-element.75), channel_id=1, source_target_pairs={{0,2},{1,3},{2,0},{3,1},{4,6},{5,7},{6,4},{7,5},{8,10},{9,11},{10,... | collective-permute-start | bytes 393224 | tf_op jit(solution)/shard_map/ppermute | solution.py:16
  83.7 7.0 %collective-permute-start.6 = (bf16[2,2,128,128]{3,2,1,0:T(8,128)(2,1)}, bf16[2,2,128,128]{3,2,1,0:T(8,128)(2,1)}, u32[]{:S(2)}, u32[]{:S(2)}) collective-permute-start(bf16[2,2,128,128]{3,2,1,0:T(8,128)(2,1)} %fusion.78), channel_id=1, source_target_pairs={{0,3},{1,2},{2,1},{3,0},{4,7},{5,6},{6,5},{7,4},{8,11},{9,10},{10,... | collective-permute-start | bytes 393224 | tf_op jit(solution)/shard_map/ppermute | solution.py:16
  85.3 7.3 %collective-permute-start.8 = (bf16[2,2,128,128]{3,2,1,0:T(8,128)(2,1)}, bf16[2,2,128,128]{3,2,1,0:T(8,128)(2,1)}, u32[]{:S(2)}, u32[]{:S(2)}) collective-permute-start(bf16[2,2,128,128]{3,2,1,0:T(8,128)(2,1)} %get-tuple-element.74), channel_id=1, source_target_pairs={{0,1},{1,0},{2,3},{3,2},{4,5},{5,4},{6,7},{7,6},{8,9},{9,8},{10,11... | collective-permute-start | bytes 393224 | tf_op jit(solution)/shard_map/ppermute | solution.py:16
  88.1 49.0 %collective-permute-start.17 = (bf16[512,1024]{1,0:T(8,128)(2,1)}, bf16[512,1024]{1,0:T(8,128)(2,1)}, u32[]{:S(2)}, u32[]{:S(2)}) collective-permute-start(bf16[512,1024]{1,0:T(8,128)(2,1)} %bitcast.202), channel_id=1, source_target_pairs={{0,1},{1,0},{2,3},{3,2},{4,5},{5,4},{6,7},{7,6},{8,9},{9,8},{10,11... | collective-permute-start | bytes 3145736 | tf_op jit(solution)/shard_map/ppermute | solution.py:16
  90.8 29.9 %collective-permute-start.13 = (bf16[352,1024]{1,0:T(8,128)(2,1)}, bf16[352,1024]{1,0:T(8,128)(2,1)}, u32[]{:S(2)}, u32[]{:S(2)}) collective-permute-start(bf16[352,1024]{1,0:T(8,128)(2,1)} %constant_dynamic-slice_fusion.2), channel_id=1, source_target_pairs={{0,2},{1,3},{2,0},{3,1},{4,6},{5,7},{6,4},{7,5},{8,10},{9,11},{10,... | collective-permute-start | bytes 2162696 | tf_op jit(solution)/shard_map/ppermute | solution.py:16
  107.0 65.6 %copy-start.86 = (bf16[2,256,1024]{2,1,0:T(8,128)(2,1)}, bf16[2,256,1024]{2,1,0:T(8,128)(2,1)S(1)}, u32[]{:S(2)}) copy-start(bf16[2,256,1024]{2,1,0:T(8,128)(2,1)S(1)} %multiply_convert_fusion.7) | copy-start | bytes 3145732
  107.1 28.1 %collective-permute-start.15 = (bf16[512,1024]{1,0:T(8,128)(2,1)S(1)}, bf16[512,1024]{1,0:T(8,128)(2,1)S(1)}, u32[]{:S(2)}, u32[]{:S(2)}) collective-permute-start(bf16[512,1024]{1,0:T(8,128)(2,1)S(1)} %bitcast.208), channel_id=1, source_target_pairs={{0,1},{1,0},{2,3},{3,2},{4,5},{5,4},{6,7},{7,6},{8,9},{9,8},{10,11... | collective-permute-start | bytes 3145736 | tf_op jit(solution)/shard_map/ppermute | solution.py:16
  120.1 21.3 %collective-permute-start.10 = (bf16[512,704]{0,1:T(8,128)(2,1)}, bf16[512,704]{0,1:T(8,128)(2,1)S(1)}, u32[]{:S(2)}, u32[]{:S(2)}) collective-permute-start(bf16[512,704]{0,1:T(8,128)(2,1)} %collective-permute-done.9), channel_id=1, source_target_pairs={{0,16},{16,0},{1,17},{17,1},{2,18},{18,2},{3,19},{19,3},{4,20},{20... | collective-permute-start | bytes 2162696 | tf_op jit(solution)/shard_map/ppermute | solution.py:16
  120.2 24.2 %collective-permute-start.12 = (bf16[512,704]{0,1:T(8,128)(2,1)}, bf16[512,704]{0,1:T(8,128)(2,1)S(1)}, u32[]{:S(2)}, u32[]{:S(2)}) collective-permute-start(bf16[512,704]{0,1:T(8,128)(2,1)} %collective-permute-done.11), channel_id=1, source_target_pairs={{0,16},{16,0},{1,17},{17,1},{2,18},{18,2},{3,19},{19,3},{4,20},{20... | collective-permute-start | bytes 2162696 | tf_op jit(solution)/shard_map/ppermute | solution.py:16
  120.7 26.3 %collective-permute-start.14 = (bf16[352,1024]{1,0:T(8,128)(2,1)}, bf16[352,1024]{1,0:T(8,128)(2,1)S(1)}, u32[]{:S(2)}, u32[]{:S(2)}) collective-permute-start(bf16[352,1024]{1,0:T(8,128)(2,1)} %collective-permute-done.13), channel_id=1, source_target_pairs={{0,16},{16,0},{1,17},{17,1},{2,18},{18,2},{3,19},{19,3},{4,20},{20... | collective-permute-start | bytes 2162696 | tf_op jit(solution)/shard_map/ppermute | solution.py:16
  135.2 37.4 %copy-start.144 = (bf16[512,1024]{1,0:T(8,128)(2,1)}, bf16[512,1024]{1,0:T(8,128)(2,1)S(1)}, u32[]{:S(2)}) copy-start(bf16[512,1024]{1,0:T(8,128)(2,1)S(1)} %collective-permute-done.15) | copy-start | bytes 3145732
  139.4 18.9 %copy-start.54 = (bf16[512,704]{0,1:T(8,128)(2,1)}, bf16[512,704]{0,1:T(8,128)(2,1)S(1)}, u32[]{:S(2)}) copy-start(bf16[512,704]{0,1:T(8,128)(2,1)S(1)} %get-tuple-element.86) | copy-start | bytes 2162692
  141.4 25.4 %copy-start.146 = (bf16[512,704]{0,1:T(8,128)(2,1)}, bf16[512,704]{0,1:T(8,128)(2,1)S(1)}, u32[]{:S(2)}) copy-start(bf16[512,704]{0,1:T(8,128)(2,1)S(1)} %collective-permute-done.10) | copy-start | bytes 2162692
  144.4 20.1 %copy-start.89 = (bf16[512,704]{0,1:T(8,128)(2,1)}, bf16[512,704]{0,1:T(8,128)(2,1)S(1)}, u32[]{:S(2)}) copy-start(bf16[512,704]{0,1:T(8,128)(2,1)S(1)} %collective-permute-done.12) | copy-start | bytes 2162692
  146.9 22.2 %copy-start.148 = (bf16[352,1024]{1,0:T(8,128)(2,1)}, bf16[352,1024]{1,0:T(8,128)(2,1)S(1)}, u32[]{:S(2)}) copy-start(bf16[352,1024]{1,0:T(8,128)(2,1)S(1)} %collective-permute-done.14) | copy-start | bytes 2162692
  156.8 76.0 %collective-permute-start.18 = (bf16[512,1024]{1,0:T(8,128)(2,1)}, bf16[512,1024]{1,0:T(8,128)(2,1)}, u32[]{:S(2)}, u32[]{:S(2)}) collective-permute-start(bf16[512,1024]{1,0:T(8,128)(2,1)} %add_convert_fusion.1), channel_id=1, source_target_pairs={{0,1},{1,0},{2,3},{3,2},{4,5},{5,4},{6,7},{7,6},{8,9},{9,8},{10,11... | collective-permute-start | bytes 3145736 | tf_op jit(solution)/shard_map/ppermute | solution.py:16
  176.9 42.4 %collective-permute-start.32 = (bf16[512,704]{0,1:T(8,128)(2,1)}, bf16[512,704]{0,1:T(8,128)(2,1)}, u32[]{:S(2)}, u32[]{:S(2)}) collective-permute-start(bf16[512,704]{0,1:T(8,128)(2,1)} %dynamic-slice_convert_fusion.2), channel_id=1, source_target_pairs={{0,16},{16,0},{1,17},{17,1},{2,18},{18,2},{3,19},{19,3},{4,20},{20... | collective-permute-start | bytes 2162696 | tf_op jit(solution)/shard_map/ppermute | solution.py:16
  179.9 47.2 %collective-permute-start.31 = (bf16[512,704]{0,1:T(8,128)(2,1)}, bf16[512,704]{0,1:T(8,128)(2,1)}, u32[]{:S(2)}, u32[]{:S(2)}) collective-permute-start(bf16[512,704]{0,1:T(8,128)(2,1)} %dynamic-slice_convert_fusion.3), channel_id=1, source_target_pairs={{0,16},{16,0},{1,17},{17,1},{2,18},{18,2},{3,19},{19,3},{4,20},{20... | collective-permute-start | bytes 2162696 | tf_op jit(solution)/shard_map/ppermute | solution.py:16
  185.3 36.4 %collective-permute-start.29 = (bf16[512,704]{0,1:T(8,128)(2,1)}, bf16[512,704]{0,1:T(8,128)(2,1)}, u32[]{:S(2)}, u32[]{:S(2)}) collective-permute-start(bf16[512,704]{0,1:T(8,128)(2,1)} %dynamic-slice_convert_fusion.4), channel_id=1, source_target_pairs={{0,16},{16,0},{1,17},{17,1},{2,18},{18,2},{3,19},{19,3},{4,20},{20... | collective-permute-start | bytes 2162696 | tf_op jit(solution)/shard_map/ppermute | solution.py:16
  196.5 28.0 %collective-permute-start.35 = (bf16[704,512]{1,0:T(8,128)(2,1)S(1)}, bf16[704,512]{1,0:T(8,128)(2,1)S(1)}, u32[]{:S(2)}, u32[]{:S(2)}) collective-permute-start(bf16[704,512]{1,0:T(8,128)(2,1)S(1)} %dynamic-slice_convert_fusion), channel_id=1, source_target_pairs={{0,16},{16,0},{1,17},{17,1},{2,18},{18,2},{3,19},{19,3},{4,20},{20... | collective-permute-start | bytes 2162696 | tf_op jit(solution)/shard_map/ppermute | solution.py:16
  219.3 10.9 %collective-permute-start.28 = (bf16[512,704]{0,1:T(8,128)(2,1)}, bf16[512,704]{0,1:T(8,128)(2,1)}, u32[]{:S(2)}, u32[]{:S(2)}) collective-permute-start(bf16[512,704]{0,1:T(8,128)(2,1)} %dynamic-slice_convert_fusion.5), channel_id=1, source_target_pairs={{0,16},{16,0},{1,17},{17,1},{2,18},{18,2},{3,19},{19,3},{4,20},{20... | collective-permute-start | bytes 2162696 | tf_op jit(solution)/shard_map/ppermute | solution.py:16
  221.7 25.8 %collective-permute-start.16 = (bf16[512,1024]{1,0:T(8,128)(2,1)}, bf16[512,1024]{1,0:T(8,128)(2,1)}, u32[]{:S(2)}, u32[]{:S(2)}) collective-permute-start(bf16[512,1024]{1,0:T(8,128)(2,1)} %add_convert_fusion.3), channel_id=1, source_target_pairs={{0,1},{1,0},{2,3},{3,2},{4,5},{5,4},{6,7},{7,6},{8,9},{9,8},{10,11... | collective-permute-start | bytes 3145736 | tf_op jit(solution)/shard_map/ppermute | solution.py:16
  224.5 74.9 %collective-permute-start.33 = (bf16[512,704]{0,1:T(8,128)(2,1)}, bf16[512,704]{0,1:T(8,128)(2,1)}, u32[]{:S(2)}, u32[]{:S(2)}) collective-permute-start(bf16[512,704]{0,1:T(8,128)(2,1)} %add_convert_fusion.8), channel_id=1, source_target_pairs={{0,2},{1,3},{2,0},{3,1},{4,6},{5,7},{6,4},{7,5},{8,10},{9,11},{10,... | collective-permute-start | bytes 2162696 | tf_op jit(solution)/shard_map/ppermute | solution.py:16
  227.1 76.1 %collective-permute-start.30 = (bf16[512,704]{0,1:T(8,128)(2,1)}, bf16[512,704]{0,1:T(8,128)(2,1)}, u32[]{:S(2)}, u32[]{:S(2)}) collective-permute-start(bf16[512,704]{0,1:T(8,128)(2,1)} %add_convert_fusion.9), channel_id=1, source_target_pairs={{0,2},{1,3},{2,0},{3,1},{4,6},{5,7},{6,4},{7,5},{8,10},{9,11},{10,... | collective-permute-start | bytes 2162696 | tf_op jit(solution)/shard_map/ppermute | solution.py:16
  270.2 8.4 %collective-permute-start.20 = (bf16[2,2,128,128]{3,2,1,0:T(8,128)(2,1)S(1)}, bf16[2,2,128,128]{3,2,1,0:T(8,128)(2,1)S(1)}, u32[]{:S(2)}, u32[]{:S(2)}) collective-permute-start(bf16[2,2,128,128]{3,2,1,0:T(8,128)(2,1)S(1)} %get-tuple-element.88), channel_id=1, source_target_pairs={{0,2},{1,3},{2,0},{3,1},{4,6},{5,7},{6,4},{7,5},{8,10},{9,11},{10,... | collective-permute-start | bytes 393224 | tf_op jit(solution)/shard_map/ppermute | solution.py:16
  271.7 7.0 %collective-permute-start.21 = (bf16[2,2,128,128]{3,2,1,0:T(8,128)(2,1)S(1)}, bf16[2,2,128,128]{3,2,1,0:T(8,128)(2,1)S(1)}, u32[]{:S(2)}, u32[]{:S(2)}) collective-permute-start(bf16[2,2,128,128]{3,2,1,0:T(8,128)(2,1)S(1)} %get-tuple-element.89), channel_id=1, source_target_pairs={{0,3},{1,2},{2,1},{3,0},{4,7},{5,6},{6,5},{7,4},{8,11},{9,10},{10,... | collective-permute-start | bytes 393224 | tf_op jit(solution)/shard_map/ppermute | solution.py:16
  272.2 7.0 %collective-permute-start.19 = (bf16[2,2,128,128]{3,2,1,0:T(8,128)(2,1)S(1)}, bf16[2,2,128,128]{3,2,1,0:T(8,128)(2,1)S(1)}, u32[]{:S(2)}, u32[]{:S(2)}) collective-permute-start(bf16[2,2,128,128]{3,2,1,0:T(8,128)(2,1)S(1)} %get-tuple-element.90), channel_id=1, source_target_pairs={{0,1},{1,0},{2,3},{3,2},{4,5},{5,4},{6,7},{7,6},{8,9},{9,8},{10,11... | collective-permute-start | bytes 393224 | tf_op jit(solution)/shard_map/ppermute | solution.py:16
  278.8 18.1 %copy-start.65 = (bf16[2,2,128,128]{3,2,1,0:T(8,128)(2,1)}, bf16[2,2,128,128]{3,2,1,0:T(8,128)(2,1)S(1)}, u32[]{:S(2)}) copy-start(bf16[2,2,128,128]{3,2,1,0:T(8,128)(2,1)S(1)} %collective-permute-done.21) | copy-start | bytes 393220
  279.4 17.5 %copy-start.97 = (f32[2]{0:T(128)S(1)}, f32[2]{0:T(128)}, u32[]{:S(2)}) copy-start(f32[2]{0:T(128)} %copy-done.96) | copy-start | bytes 28
  279.4 17.5 %copy-start.100 = (f32[2]{0:T(128)S(1)}, f32[2]{0:T(128)}, u32[]{:S(2)}) copy-start(f32[2]{0:T(128)} %copy-done.99) | copy-start | bytes 28
  279.4 17.5 %copy-start.104 = (f32[2]{0:T(128)S(1)}, f32[2]{0:T(128)}, u32[]{:S(2)}) copy-start(f32[2]{0:T(128)} %copy-done.103) | copy-start | bytes 28
  279.4 17.5 %copy-start.106 = (f32[2]{0:T(128)S(1)}, f32[2]{0:T(128)}, u32[]{:S(2)}) copy-start(f32[2]{0:T(128)} %copy-done.105) | copy-start | bytes 28
  279.4 17.5 %copy-start.112 = (f32[2]{0:T(128)S(1)}, f32[2]{0:T(128)}, u32[]{:S(2)}) copy-start(f32[2]{0:T(128)} %copy-done.111) | copy-start | bytes 28
  279.4 17.5 %copy-start.114 = (f32[2]{0:T(128)S(1)}, f32[2]{0:T(128)}, u32[]{:S(2)}) copy-start(f32[2]{0:T(128)} %copy-done.113) | copy-start | bytes 28
  279.4 17.5 %copy-start.119 = (f32[2]{0:T(128)S(1)}, f32[2]{0:T(128)}, u32[]{:S(2)}) copy-start(f32[2]{0:T(128)} %get-tuple-element.108) | copy-start | bytes 28
  279.5 17.5 %copy-start.120 = (f32[2]{0:T(128)S(1)}, f32[2]{0:T(128)}, u32[]{:S(2)}) copy-start(f32[2]{0:T(128)} %get-tuple-element.109) | copy-start | bytes 28
  279.5 17.5 %copy-start.122 = (f32[2]{0:T(128)S(1)}, f32[2]{0:T(128)}, u32[]{:S(2)}) copy-start(f32[2]{0:T(128)} %copy-done.121) | copy-start | bytes 28
  279.5 19.0 %copy-start.116 = (f32[2]{0:T(128)S(1)}, f32[2]{0:T(128)}, u32[]{:S(2)}) copy-start(f32[2]{0:T(128)} %copy-done.115) | copy-start | bytes 28
  279.5 19.0 %copy-start.118 = (f32[2]{0:T(128)S(1)}, f32[2]{0:T(128)}, u32[]{:S(2)}) copy-start(f32[2]{0:T(128)} %copy-done.117) | copy-start | bytes 28
  279.5 19.0 %copy-start.131 = (f32[2]{0:T(128)S(1)}, f32[2]{0:T(128)}, u32[]{:S(2)}) copy-start(f32[2]{0:T(128)} %get-tuple-element.113) | copy-start | bytes 28
  279.5 19.0 %copy-start.135 = (f32[2]{0:T(128)S(1)}, f32[2]{0:T(128)}, u32[]{:S(2)}) copy-start(f32[2]{0:T(128)} %copy-done.134) | copy-start | bytes 28
  279.5 10.5 %collective-permute-start.24 = (bf16[2,2,128,128]{3,2,1,0:T(8,128)(2,1)S(1)}, bf16[2,2,128,128]{3,2,1,0:T(8,128)(2,1)S(1)}, u32[]{:S(2)}, u32[]{:S(2)}) collective-permute-start(bf16[2,2,128,128]{3,2,1,0:T(8,128)(2,1)S(1)} %fusion.92), channel_id=1, source_target_pairs={{12,0},{13,1},{14,2},{15,3},{28,16},{29,17},{30,18},{31,19}} | collective-permute-start | bytes 393224 | tf_op jit(solution)/shard_map/ppermute | solution.py:23
  280.8 14.5 %collective-permute-start.23 = (bf16[2,2,128,128]{3,2,1,0:T(8,128)(2,1)S(1)}, bf16[2,2,128,128]{3,2,1,0:T(8,128)(2,1)S(1)}, u32[]{:S(2)}, u32[]{:S(2)}) collective-permute-start(bf16[2,2,128,128]{3,2,1,0:T(8,128)(2,1)S(1)} %fusion.92), channel_id=1, source_target_pairs={{8,0},{12,4},{9,1},{13,5},{10,2},{14,6},{11,3},{15,7},{24,16},{28,... | collective-permute-start | bytes 393224 | tf_op jit(solution)/shard_map/ppermute | solution.py:23
  282.1 14.8 %collective-permute-start.22 = (bf16[2,2,128,128]{3,2,1,0:T(8,128)(2,1)S(1)}, bf16[2,2,128,128]{3,2,1,0:T(8,128)(2,1)S(1)}, u32[]{:S(2)}, u32[]{:S(2)}) collective-permute-start(bf16[2,2,128,128]{3,2,1,0:T(8,128)(2,1)S(1)} %fusion.92), channel_id=1, source_target_pairs={{4,0},{8,4},{12,8},{5,1},{9,5},{13,9},{6,2},{10,6},{14,10},{7,3},{... | collective-permute-start | bytes 393224 | tf_op jit(solution)/shard_map/ppermute | solution.py:23
  290.1 20.6 %collective-permute-start.34 = (bf16[704,512]{1,0:T(8,128)(2,1)}, bf16[704,512]{1,0:T(8,128)(2,1)}, u32[]{:S(2)}, u32[]{:S(2)}) collective-permute-start(bf16[704,512]{1,0:T(8,128)(2,1)} %dynamic-slice_convert_fusion.1), channel_id=1, source_target_pairs={{0,16},{16,0},{1,17},{17,1},{2,18},{18,2},{3,19},{19,3},{4,20},{20... | collective-permute-start | bytes 2162696 | tf_op jit(solution)/shard_map/ppermute | solution.py:16
  295.3 22.1 %collective-permute-start.36 = (bf16[704,512]{1,0:T(8,128)(2,1)}, bf16[704,512]{1,0:T(8,128)(2,1)}, u32[]{:S(2)}, u32[]{:S(2)}) collective-permute-start(bf16[704,512]{1,0:T(8,128)(2,1)} %add_convert_fusion.7), channel_id=1, source_target_pairs={{0,2},{1,3},{2,0},{3,1},{4,6},{5,7},{6,4},{7,5},{8,10},{9,11},{10,... | collective-permute-start | bytes 2162696 | tf_op jit(solution)/shard_map/ppermute | solution.py:16
  298.0 23.5 %collective-permute-start.26 = (bf16[2,2,128,128]{3,2,1,0:T(8,128)(2,1)}, bf16[2,2,128,128]{3,2,1,0:T(8,128)(2,1)}, u32[]{:S(2)}, u32[]{:S(2)}) collective-permute-start(bf16[2,2,128,128]{3,2,1,0:T(8,128)(2,1)} %get-tuple-element.73), channel_id=1, source_target_pairs={{0,2},{1,3},{2,0},{3,1},{4,6},{5,7},{6,4},{7,5},{8,10},{9,11},{10,... | collective-permute-start | bytes 393224 | tf_op jit(solution)/shard_map/ppermute | solution.py:16
  299.4 22.1 %collective-permute-start.25 = (bf16[2,2,128,128]{3,2,1,0:T(8,128)(2,1)}, bf16[2,2,128,128]{3,2,1,0:T(8,128)(2,1)}, u32[]{:S(2)}, u32[]{:S(2)}) collective-permute-start(bf16[2,2,128,128]{3,2,1,0:T(8,128)(2,1)} %fusion.95), channel_id=1, source_target_pairs={{0,3},{1,2},{2,1},{3,0},{4,7},{5,6},{6,5},{7,4},{8,11},{9,10},{10,... | collective-permute-start | bytes 393224 | tf_op jit(solution)/shard_map/ppermute | solution.py:16
  303.3 18.2 %collective-permute-start.27 = (bf16[2,2,128,128]{3,2,1,0:T(8,128)(2,1)}, bf16[2,2,128,128]{3,2,1,0:T(8,128)(2,1)}, u32[]{:S(2)}, u32[]{:S(2)}) collective-permute-start(bf16[2,2,128,128]{3,2,1,0:T(8,128)(2,1)} %get-tuple-element.72), channel_id=1, source_target_pairs={{0,1},{1,0},{2,3},{3,2},{4,5},{5,4},{6,7},{7,6},{8,9},{9,8},{10,11... | collective-permute-start | bytes 393224 | tf_op jit(solution)/shard_map/ppermute | solution.py:16
  (130 other events, 618.9 us)
